TPU v7x, 32 devices: a whole 2x2x4 slice. The times are simulated.
32 devices in a mesh: dp: 8 (over z, y), dap: 4 (over x, core).
Axes of the slice: x: 2, y: 2, z: 4, core: 2. Of those that a mesh axis runs over, the one named last changes fastest.
Arguments:
- single_rep: bfloat16 [8, 128, 384], P('dp', 'dap')
- pair_rep: bfloat16 [8, 128, 128, 256], P('dp', 'dap')
- token_mask: int32 [8, 128], P('dp')
- d_single_out: bfloat16 [8, 128, 384], P('dp', 'dap')
- d_pair_out: bfloat16 [8, 128, 128, 256], P('dp', 'dap')
- mul_out_in: bfloat16 [256, 1024], replicated
- mul_out_gate: bfloat16 [256, 256], replicated
- mul_out_proj: bfloat16 [256, 256], replicated
- mul_in_in: bfloat16 [256, 1024], replicated
- mul_in_gate: bfloat16 [256, 256], replicated
- mul_in_proj: bfloat16 [256, 256], replicated
- att_st_qkvg: bfloat16 [256, 1024], replicated
- att_st_bias: bfloat16 [256, 8], replicated
- att_st_proj: bfloat16 [256, 256], replicated
- att_en_qkvg: bfloat16 [256, 1024], replicated
- att_en_bias: bfloat16 [256, 8], replicated
- att_en_proj: bfloat16 [256, 256], replicated
- pair_up: bfloat16 [256, 2048], replicated
- pair_down: bfloat16 [1024, 256], replicated
- sing_qkvg: bfloat16 [384, 1536], replicated
- sing_qbias: bfloat16 [384], replicated
- sing_pbias: bfloat16 [256, 16], replicated
- sing_proj: bfloat16 [384, 384], replicated
- sing_up: bfloat16 [384, 3072], replicated
- sing_down: bfloat16 [1536, 384], replicated
Outputs:
- output 1: bfloat16 [8, 128, 384], P('dp', 'dap')
- output 2: bfloat16 [8, 128, 128, 256], P('dp', 'dap')
- output 3: bfloat16 [8, 128, 384], P('dp', 'dap')
- output 4: bfloat16 [8, 128, 128, 256], P('dp', 'dap')
- output 5: float32 [4743552], P('dp')
All inputs are finite; a program needn't handle non-finite values.
Results may differ from a plain program's by a relative error of at most 0.02.
Values are sent between devices in bfloat16 or wider.
A program may use at most 1 GiB of HBM per device.

v0:
```python
import functools
import jax
import jax.numpy as jnp
from jax import lax
from jax.sharding import PartitionSpec as P

BATCH_AXIS = 'dp'
GROUP_AXIS = 'dap'
NORM_EPS = 1e-5
MASK_PENALTY = 1.0e9


def layer_norm(x_in):
    x_f32 = x_in.astype(jnp.float32)
    centered = x_f32 - jnp.mean(x_f32, axis=-1, keepdims=True)
    row_var = jnp.mean(centered * centered, axis=-1, keepdims=True)
    return centered * lax.rsqrt(row_var + NORM_EPS)


def mul_pre(z_rows, w_in, w_gate):
    normed = layer_norm(z_rows).astype(jnp.bfloat16)
    proj_all = jnp.dot(normed, w_in, preferred_element_type=jnp.float32)
    inner_dim = w_in.shape[1] // 4
    left_proj = (jax.nn.sigmoid(proj_all[..., inner_dim:2 * inner_dim]) * proj_all[..., :inner_dim]).astype(jnp.bfloat16)
    right_proj = (jax.nn.sigmoid(proj_all[..., 3 * inner_dim:]) * proj_all[..., 2 * inner_dim:3 * inner_dim]).astype(jnp.bfloat16)
    gate_vals = jax.nn.sigmoid(jnp.dot(normed, w_gate, preferred_element_type=jnp.float32))
    return left_proj, right_proj, gate_vals


def mul_post(z_rows, mixed_sum, gate_vals, w_out):
    normed = layer_norm(mixed_sum).astype(jnp.bfloat16)
    update = gate_vals * jnp.dot(normed, w_out, preferred_element_type=jnp.float32)
    return (z_rows.astype(jnp.float32) + update).astype(jnp.bfloat16)


def att_pre(z_rows, w_qkvg, w_tb):
    normed = layer_norm(z_rows).astype(jnp.bfloat16)
    proj_all = jnp.dot(normed, w_qkvg, preferred_element_type=jnp.float32)
    inner_dim = w_qkvg.shape[1] // 4
    num_heads = w_tb.shape[1]
    head_shape = z_rows.shape[:2] + (num_heads, inner_dim // num_heads)
    q_rows = proj_all[..., :inner_dim].astype(jnp.bfloat16).reshape(head_shape)
    k_rows = proj_all[..., inner_dim:2 * inner_dim].astype(jnp.bfloat16).reshape(head_shape)
    v_rows = proj_all[..., 2 * inner_dim:3 * inner_dim].astype(jnp.bfloat16).reshape(head_shape)
    gate_vals = jax.nn.sigmoid(proj_all[..., 3 * inner_dim:])
    bias_rows = jnp.dot(normed, w_tb, preferred_element_type=jnp.float32).astype(jnp.bfloat16)
    return q_rows, k_rows, v_rows, gate_vals, bias_rows


def att_core(q_rows, k_rows, v_rows, bias_full, mask_bias):
    att_scale = q_rows.shape[-1] ** -0.5
    logits = jnp.einsum('ijhd,ikhd->ihjk', q_rows, k_rows, preferred_element_type=jnp.float32) * att_scale
    logits = logits + jnp.transpose(bias_full, (2, 0, 1)) + mask_bias
    prob_mat = jax.nn.softmax(logits, axis=-1).astype(jnp.bfloat16)
    return jnp.einsum('ihjk,ikhd->ijhd', prob_mat, v_rows, preferred_element_type=jnp.float32)


def gated_out(x_rows, attended, gate_vals, w_o):
    gated = (gate_vals * attended.reshape(gate_vals.shape)).astype(jnp.bfloat16)
    return (x_rows.astype(jnp.float32) + jnp.dot(gated, w_o, preferred_element_type=jnp.float32)).astype(jnp.bfloat16)


def transition(x_rows, w_up, w_down):
    normed = layer_norm(x_rows).astype(jnp.bfloat16)
    hidden = jnp.dot(normed, w_up, preferred_element_type=jnp.float32)
    inner_dim = w_down.shape[0]
    acted = (jax.nn.silu(hidden[..., :inner_dim]) * hidden[..., inner_dim:]).astype(jnp.bfloat16)
    return (x_rows.astype(jnp.float32) + jnp.dot(acted, w_down, preferred_element_type=jnp.float32)).astype(jnp.bfloat16)


def single_pre(s_rows, w_qkvg, q_bias):
    normed = layer_norm(s_rows).astype(jnp.bfloat16)
    proj_all = jnp.dot(normed, w_qkvg, preferred_element_type=jnp.float32)
    inner_dim = w_qkvg.shape[1] // 4
    q_rows = (proj_all[:, :inner_dim] + q_bias.astype(jnp.float32)).astype(jnp.bfloat16)
    k_rows = proj_all[:, inner_dim:2 * inner_dim].astype(jnp.bfloat16)
    v_rows = proj_all[:, 2 * inner_dim:3 * inner_dim].astype(jnp.bfloat16)
    gate_vals = jax.nn.sigmoid(proj_all[:, 3 * inner_dim:])
    return q_rows, k_rows, v_rows, gate_vals


def pair_bias(z_rows, w_pb):
    normed = layer_norm(z_rows).astype(jnp.bfloat16)
    return jnp.dot(normed, w_pb, preferred_element_type=jnp.float32).astype(jnp.bfloat16)


def single_core(q_rows, k_all, v_all, bias_rows, mask_bias):
    num_heads = bias_rows.shape[-1]
    head_dim = q_rows.shape[-1] // num_heads
    q_heads = q_rows.reshape(q_rows.shape[0], num_heads, head_dim)
    k_heads = k_all.reshape(k_all.shape[0], num_heads, head_dim)
    v_heads = v_all.reshape(v_all.shape[0], num_heads, head_dim)
    logits = jnp.einsum('ihd,jhd->hij', q_heads, k_heads, preferred_element_type=jnp.float32) * head_dim ** -0.5
    logits = logits + jnp.transpose(bias_rows, (2, 0, 1)).astype(jnp.float32) + mask_bias
    prob_mat = jax.nn.softmax(logits, axis=-1).astype(jnp.bfloat16)
    return jnp.einsum('hij,jhd->ihd', prob_mat, v_heads, preferred_element_type=jnp.float32)


def gather_rows(x_in):
    return lax.all_gather(x_in, GROUP_AXIS, axis=0, tiled=True)


def scatter_rows(x_in):
    return lax.psum_scatter(x_in, GROUP_AXIS, scatter_dimension=0, tiled=True)


def rows_to_cols(x_in):
    return jnp.transpose(lax.all_to_all(x_in, GROUP_AXIS, 1, 0, tiled=True), (1, 0, 2))


def cols_to_rows(x_in):
    return lax.all_to_all(jnp.transpose(x_in, (1, 0, 2)), GROUP_AXIS, 0, 1, tiled=True)


def mul_out_forward(z_rows, w_in, w_gate, w_out):
    (left_proj, right_proj, gate_vals), pull_pre = jax.vjp(mul_pre, z_rows, w_in, w_gate)
    right_all = gather_rows(right_proj)
    mixed_sum = jnp.einsum('ikc,jkc->ijc', left_proj, right_all, preferred_element_type=jnp.float32)
    z_new, pull_post = jax.vjp(mul_post, z_rows, mixed_sum, gate_vals, w_out)
    return z_new, (pull_pre, pull_post, left_proj, right_all)


def mul_out_backward(dz_new, saved_state):
    pull_pre, pull_post, left_proj, right_all = saved_state
    dz_post, d_mixed, d_gate, g_out = pull_post(dz_new)
    d_mixed = d_mixed.astype(jnp.bfloat16)
    d_left = jnp.einsum('ijc,jkc->ikc', d_mixed, right_all, preferred_element_type=jnp.float32).astype(jnp.bfloat16)
    right_part = jnp.einsum('ijc,ikc->jkc', d_mixed, left_proj, preferred_element_type=jnp.float32)
    d_right = scatter_rows(right_part).astype(jnp.bfloat16)
    dz_pre, g_in, g_gate = pull_pre((d_left, d_right, d_gate))
    return dz_post + dz_pre, [g_in, g_gate, g_out]


def mul_in_forward(z_rows, w_in, w_gate, w_out):
    (left_proj, right_proj, gate_vals), pull_pre = jax.vjp(mul_pre, z_rows, w_in, w_gate)
    left_cols = lax.all_to_all(left_proj, GROUP_AXIS, 1, 0, tiled=True)
    right_all = gather_rows(right_proj)
    mixed_sum = jnp.einsum('kic,kjc->ijc', left_cols, right_all, preferred_element_type=jnp.float32)
    z_new, pull_post = jax.vjp(mul_post, z_rows, mixed_sum, gate_vals, w_out)
    return z_new, (pull_pre, pull_post, left_cols, right_all)


def mul_in_backward(dz_new, saved_state):
    pull_pre, pull_post, left_cols, right_all = saved_state
    dz_post, d_mixed, d_gate, g_out = pull_post(dz_new)
    d_mixed = d_mixed.astype(jnp.bfloat16)
    d_left_cols = jnp.einsum('ijc,kjc->kic', d_mixed, right_all, preferred_element_type=jnp.float32).astype(jnp.bfloat16)
    d_left = lax.all_to_all(d_left_cols, GROUP_AXIS, 0, 1, tiled=True)
    right_part = jnp.einsum('ijc,kic->kjc', d_mixed, left_cols, preferred_element_type=jnp.float32)
    d_right = scatter_rows(right_part).astype(jnp.bfloat16)
    dz_pre, g_in, g_gate = pull_pre((d_left, d_right, d_gate))
    return dz_post + dz_pre, [g_in, g_gate, g_out]


def att_forward(z_rows, mask_bias, w_qkvg, w_tb, w_o):
    (q_rows, k_rows, v_rows, gate_vals, bias_rows), pull_pre = jax.vjp(att_pre, z_rows, w_qkvg, w_tb)
    bias_full = gather_rows(bias_rows).astype(jnp.float32)
    attended, pull_core = jax.vjp(functools.partial(att_core, mask_bias=mask_bias), q_rows, k_rows, v_rows, bias_full)
    z_new, pull_post = jax.vjp(gated_out, z_rows, attended, gate_vals, w_o)
    return z_new, (pull_pre, pull_core, pull_post)


def att_backward(dz_new, saved_state):
    pull_pre, pull_core, pull_post = saved_state
    dz_post, d_att, d_gate, g_out = pull_post(dz_new)
    d_query, d_key, d_value, d_bias_full = pull_core(d_att)
    d_bias = scatter_rows(d_bias_full).astype(jnp.bfloat16)
    dz_pre, g_qkvg, g_bias = pull_pre((d_query, d_key, d_value, d_gate, d_bias))
    return dz_post + dz_pre, [g_qkvg, g_bias, g_out]


def single_forward(s_rows, z_rows, mask_bias, w_qkvg, q_bias, w_pb, w_o, w_up, w_down):
    (q_rows, k_rows, v_rows, gate_vals), pull_pre = jax.vjp(single_pre, s_rows, w_qkvg, q_bias)
    bias_rows, pull_bias = jax.vjp(pair_bias, z_rows, w_pb)
    k_all = gather_rows(k_rows)
    v_all = gather_rows(v_rows)
    attended, pull_core = jax.vjp(functools.partial(single_core, mask_bias=mask_bias), q_rows, k_all, v_all, bias_rows)
    s_mid, pull_post = jax.vjp(gated_out, s_rows, attended, gate_vals, w_o)
    s_new, pull_trans = jax.vjp(transition, s_mid, w_up, w_down)
    return s_new, (pull_pre, pull_bias, pull_core, pull_post, pull_trans)


def single_backward(ds_new, saved_state):
    pull_pre, pull_bias, pull_core, pull_post, pull_trans = saved_state
    ds_mid, g_up, g_down = pull_trans(ds_new)
    ds_post, d_att, d_gate, g_out = pull_post(ds_mid)
    d_query, d_key_all, d_value_all, d_bias_rows = pull_core(d_att)
    d_key = scatter_rows(d_key_all.astype(jnp.float32)).astype(jnp.bfloat16)
    d_value = scatter_rows(d_value_all.astype(jnp.float32)).astype(jnp.bfloat16)
    ds_pre, g_qkvg, g_qbias = pull_pre((d_query, d_key, d_value, d_gate))
    dz_bias, g_pbias = pull_bias(d_bias_rows)
    return ds_post + ds_pre, dz_bias, [g_qkvg, g_qbias, g_pbias, g_out, g_up, g_down]


def device_step(single_blk, pair_blk, mask_blk, d_single_blk, d_pair_blk, *weights):
    s_rows = single_blk[0]
    z_rows = pair_blk[0]
    mask_bias = (mask_blk[0].astype(jnp.float32) - 1.0) * MASK_PENALTY
    z_one, saved_one = mul_out_forward(z_rows, weights[0], weights[1], weights[2])
    z_two, saved_two = mul_in_forward(z_one, weights[3], weights[4], weights[5])
    z_three, saved_three = att_forward(z_two, mask_bias, weights[6], weights[7], weights[8])
    zt_four, saved_four = att_forward(rows_to_cols(z_three), mask_bias, weights[9], weights[10], weights[11])
    z_four = cols_to_rows(zt_four)
    z_five, pull_pair = jax.vjp(transition, z_four, weights[12], weights[13])
    s_out, saved_single = single_forward(s_rows, z_five, mask_bias, *weights[14:20])
    ds_in, dz_bias, single_grads = single_backward(d_single_blk[0], saved_single)
    dz_four, g_pup, g_pdown = pull_pair(d_pair_blk[0] + dz_bias)
    dzt_three, end_grads = att_backward(rows_to_cols(dz_four), saved_four)
    dz_two, start_grads = att_backward(cols_to_rows(dzt_three), saved_three)
    dz_one, in_grads = mul_in_backward(dz_two, saved_two)
    dz_zero, out_grads = mul_out_backward(dz_one, saved_one)
    all_grads = out_grads + in_grads + start_grads + end_grads + [g_pup, g_pdown] + single_grads
    grad_flat = jnp.concatenate([g_item.astype(jnp.float32).reshape(-1) for g_item in all_grads])
    grad_flat = lax.psum(grad_flat, GROUP_AXIS)
    grad_flat = lax.psum_scatter(grad_flat, BATCH_AXIS, scatter_dimension=0, tiled=True)
    return s_out[None], z_five[None], ds_in[None], dz_zero[None], grad_flat


def solution(mesh):
    spec_single = P(BATCH_AXIS, GROUP_AXIS, None)
    spec_pair = P(BATCH_AXIS, GROUP_AXIS, None, None)
    spec_mask = P(BATCH_AXIS, None)

    def block_fn(single_rep, pair_rep, token_mask, d_single_out, d_pair_out, *weights):
        in_specs = (spec_single, spec_pair, spec_mask, spec_single, spec_pair) + tuple(P() for w_item in weights)
        out_specs = (spec_single, spec_pair, spec_single, spec_pair, P(BATCH_AXIS))
        mapped = jax.shard_map(device_step, mesh=mesh, in_specs=in_specs, out_specs=out_specs, check_vma=False)
        return mapped(single_rep, pair_rep, token_mask, d_single_out, d_pair_out, *weights)

    return block_fn
```

profile of v0, /device:TPU:0, one launch (start us, length us, event | category | flops | bytes accessed | tf_op | source)
XLA Modules:
  0.0 2133.6 jit_solution(11678908415152228017)
XLA Ops:
  26.9 56.3 %all-gather.3.cloned.1.call-done = bf16[128,128,256]{2,1,0:T(8,128)(2,1)} async-done(((bf16[32,128,256]{2,1,0:T(8,128)(2,1)}), bf16[128,128,256]{2,1,0:T(8,128)(2,1)}) %all-gather.3.cloned.1.call-update) | async-done | bytes 8388624 | tf_op jit(solution)/shard_map/all_gather | solution.py:100
  83.2 12.4 copy.370
  133.2 47.8 %all-to-all-done = bf16[32,128,256]{2,0,1:T(8,128)(2,1)} async-done(((bf16[32,128,256]{2,0,1:T(8,128)(2,1)}), bf16[32,128,256]{2,0,1:T(8,128)(2,1)}, u32[]{:S(2)}, u32[]{:S(2)}) %all-to-all-start) | async-done | bytes 2097184 | tf_op jit(solution)/shard_map/all_to_all | solution.py:136
  190.3 14.9 all-gather.5.cloned.1.call-done
  205.2 12.4 copy.376
  267.7 11.3 fusion.390
  303.1 28.3 %all_to_all.81 = bf16[32,128,256]{2,0,1:T(8,128)(2,1)S(1)} all-to-all(bf16[32,128,256]{2,0,1:T(8,128)(2,1)S(1)} %copy.385), channel_id=1, replica_groups=mesh['dp'=8,'dap'=4] {'dap'}, dimensions={1} | all-to-all | bytes 4194304 | tf_op jit(solution)/shard_map/all_to_all | solution.py:108
  371.4 11.3 fusion.392
  419.4 20.5 all_gather.19
  465.1 13.1 fusion.230
  478.3 13.2 multiply_convert_fusion
  523.2 27.3 %convert_multiply_fusion.3 = (f32[32,128,1024]{2,1,0:T(8,128)}, f32[32,128,1024]{2,1,0:T(8,128)}) fusion(f32[32,128,2048]{2,1,0:T(8,128)} %fusion.230, bf16[32,128,256]{2,1,0:T(8,128)(2,1)} %fusion.136, bf16[1024,256]{1,0:T(8,128)(2,1)} %param.43), kind=kOutput, calls=%fused_computation.11 | convolution fusion | flops 2206203904 | bytes 69730304 | tf_op jit(solution)/shard_map/transpose(jvp())/dot_general | solution.py:68
  550.6 13.9 fusion.73
  578.2 25.3 %all-to-all-done.3 = bf16[32,128,256]{2,0,1:T(8,128)(2,1)S(1)} async-done(((bf16[32,128,256]{2,0,1:T(8,128)(2,1)}), bf16[32,128,256]{2,0,1:T(8,128)(2,1)S(1)}, u32[]{:S(2)}, u32[]{:S(2)}) %all-to-all-start.3) | async-done | bytes 2097184 | tf_op jit(solution)/shard_map/all_to_all | solution.py:108
  617.7 13.4 fusion.7
  631.1 12.6 fusion.144
  713.5 25.3 %all-to-all-done.4 = bf16[128,32,256]{2,1,0:T(8,128)(2,1)S(1)} async-done(((bf16[128,32,256]{2,1,0:T(8,128)(2,1)}), bf16[128,32,256]{2,1,0:T(8,128)(2,1)S(1)}, u32[]{:S(2)}, u32[]{:S(2)}) %all-to-all-start.4) | async-done | bytes 2097184 | tf_op jit(solution)/shard_map/all_to_all | solution.py:112
  752.6 13.4 fusion.11
  766.0 12.6 fusion.150
  860.9 17.9 copy.431
  907.3 28.2 %all-to-all-done.5 = bf16[128,32,256]{2,1,0:T(8,128)(2,1)} async-done(((bf16[128,32,256]{2,1,0:T(8,128)(2,1)}), bf16[128,32,256]{2,1,0:T(8,128)(2,1)}, u32[]{:S(2)}, u32[]{:S(2)}) %all-to-all-start.5) | async-done | bytes 2097184 | tf_op jit(solution)/shard_map/all_to_all | solution.py:148
  939.9 75.1 %reduce-scatter.15.cloned.1.call-done = f32[32,128,256]{2,1,0:T(8,128)} async-done(((f32[128,128,256]{2,1,0:T(8,128)}), f32[32,128,256]{2,1,0:T(8,128)}) %reduce-scatter.15.cloned.1.call-update) | async-done | bytes 4194320 | tf_op jit(solution)/shard_map/reduce_scatter | solution.py:104
  1015.0 15.9 convert_multiply_fusion.16
  1030.9 9.8 fusion.85
  1076.4 17.8 copy.437
  1117.2 12.7 fusion.170
  1218.7 15.1 convert_multiply_fusion.9
  1278.6 36.5 %dynamic-update-slice.18 = bf16[4743552]{0:T(1024)(128)(2,1)} dynamic-update-slice(bf16[4743552]{0:T(1024)(128)(2,1)} %dynamic-update-slice.17, bf16[1179648]{0:T(1024)(128)(2,1)S(1)} %bitcast.632, s32[]{} %constant.152) | dynamic-update-slice | bytes 4718596
  1315.1 18.8 dynamic-update-slice.19
  1333.9 731.1 %all-reduce.29 = f32[4743552]{0:T(1024)} all-reduce(bf16[4743552]{0:T(1024)(128)(2,1)} %dynamic-update-slice.19), channel_id=8, replica_groups=mesh['dp'=8,'dap'=4] {'dp'}, use_global_device_ids=true, to_apply=%region_59.60.clone | all-reduce | flops 4743552 | bytes 28461312
  2069.2 10.5 fusion.141
  2079.7 43.9 %all-reduce.28.cloned.1.call-done = f32[592944]{0:T(1024)} async-done(((f32[592944]{0:T(1024)}), f32[592944]{0:T(1024)}) %all-reduce.28.cloned.1.call-update) | async-done | bytes 2371792 | tf_op jit(solution)/shard_map/psum | solution.py:214
  (806 shorter events, 696.6 us)
Async XLA Ops:
  7.2 496.9 %copy-start = (bf16[384,3072]{1,0:T(8,128)(2,1)S(1)}, bf16[384,3072]{1,0:T(8,128)(2,1)}, u32[]{:S(2)}) copy-start(bf16[384,3072]{1,0:T(8,128)(2,1)} %param.48) | copy-start | bytes 7077892
  7.2 76.0 %all-gather.3.cloned.1.call-start = ((), (), s32[]{:S(2)}) async-start(), calls=%async_computation.12 | async-start | bytes 10485760 | tf_op jit(solution)/shard_map/all_gather | solution.py:100
  9.6 99.6 %copy-start.117 = (f32[32,128]{1,0:T(8,128)}, f32[32,128]{1,0:T(8,128)S(1)}, u32[]{:S(2)}) copy-start(f32[32,128]{1,0:T(8,128)S(1)} %broadcast_multiply_fusion.7) | copy-start | bytes 49156
  12.2 97.0 %copy-start.153 = (f32[32,128]{1,0:T(8,128)}, f32[32,128]{1,0:T(8,128)S(1)}, u32[]{:S(2)}) copy-start(f32[32,128]{1,0:T(8,128)S(1)} %fusion.321) | copy-start | bytes 49156
  21.8 183.4 %all-gather.5.cloned.1.call-start = ((), (), s32[]{:S(2)}) async-start(), calls=%async_computation.13 | async-start | bytes 10485760 | tf_op jit(solution)/shard_map/all_gather | solution.py:100
  113.6 115.5 %copy-start.102 = (f32[32,128]{1,0:T(8,128)}, f32[32,128]{1,0:T(8,128)S(1)}, u32[]{:S(2)}) copy-start(f32[32,128]{1,0:T(8,128)S(1)} %broadcast_multiply_fusion.5) | copy-start | bytes 49156
  115.0 114.1 %copy-start.120 = (f32[32,128]{1,0:T(8,128)}, f32[32,128]{1,0:T(8,128)S(1)}, u32[]{:S(2)}) copy-start(f32[32,128]{1,0:T(8,128)S(1)} %fusion.323) | copy-start | bytes 49156
  128.5 52.5 %all-to-all-start = ((bf16[32,128,256]{2,0,1:T(8,128)(2,1)}), bf16[32,128,256]{2,0,1:T(8,128)(2,1)}, u32[]{:S(2)}, u32[]{:S(2)}) async-start(bf16[32,128,256]{2,0,1:T(8,128)(2,1)} %copy.373), calls=%async_computation | async-start | bytes 4194304 | tf_op jit(solution)/shard_map/all_to_all | solution.py:136
  133.2 238.2 %copy-start.239 = (f32[128]{0:T(128)}, f32[128]{0:T(128)S(1)}, u32[]{:S(2)}) copy-start(f32[128]{0:T(128)S(1)} %multiply_bitcast_fusion.1) | copy-start | bytes 1540
  408.7 38.5 %all-to-all-start.2 = ((bf16[128,32,256]{2,1,0:T(8,128)(2,1)}), bf16[128,32,256]{2,1,0:T(8,128)(2,1)}, u32[]{:S(2)}, u32[]{:S(2)}) async-start(bf16[128,32,256]{2,1,0:T(8,128)(2,1)} %copy.393), calls=%async_computation.2 | async-start | bytes 4194304 | tf_op jit(solution)/shard_map/all_to_all | solution.py:112
  494.9 24.7 %copy-start.151 = (f32[32,128]{1,0:T(8,128)}, f32[32,128]{1,0:T(8,128)S(1)}, u32[]{:S(2)}) copy-start(f32[32,128]{1,0:T(8,128)S(1)} %broadcast_multiply_fusion.1) | copy-start | bytes 49156
  523.2 27.3 %copy-start.27 = (f32[32,4,32,256]{3,2,1,0:T(8,128)S(1)}, f32[32,4,32,256]{3,2,1,0:T(8,128)}, u32[]{:S(2)}) copy-start(f32[32,4,32,256]{3,2,1,0:T(8,128)} %copy.395) | copy-start | bytes 12582916
  523.2 27.3 %copy-start.99 = (bf16[256,2048]{1,0:T(8,128)(2,1)S(1)}, bf16[256,2048]{1,0:T(8,128)(2,1)}, u32[]{:S(2)}) copy-start(bf16[256,2048]{1,0:T(8,128)(2,1)} %param.42) | copy-start | bytes 3145732
  523.2 27.4 %copy-start.172 = (f32[32,128]{1,0:T(8,128)S(1)}, f32[32,128]{1,0:T(8,128)}, u32[]{:S(2)}) copy-start(f32[32,128]{1,0:T(8,128)} %copy-done.171) | copy-start | bytes 49156
  574.4 33.6 %copy-start.210 = (bf16[256,256]{1,0:T(8,128)(2,1)S(1)}, bf16[256,256]{1,0:T(8,128)(2,1)}, u32[]{:S(2)}) copy-start(bf16[256,256]{1,0:T(8,128)(2,1)} %param.41) | copy-start | bytes 393220
  574.4 29.2 %all-to-all-start.3 = ((bf16[32,128,256]{2,0,1:T(8,128)(2,1)}), bf16[32,128,256]{2,0,1:T(8,128)(2,1)S(1)}, u32[]{:S(2)}, u32[]{:S(2)}) async-start(bf16[32,128,256]{2,0,1:T(8,128)(2,1)} %copy.407), calls=%async_computation.5 | async-start | bytes 4194304 | tf_op jit(solution)/shard_map/all_to_all | solution.py:108
  578.1 112.2 %reduce-scatter.11.cloned.1.call-start = ((), (), s32[]{:S(2)}) async-start(), calls=%async_computation.16 | async-start | bytes 655360 | tf_op jit(solution)/shard_map/reduce_scatter | solution.py:104
  709.6 32.4 %copy-start.218 = (bf16[256,256]{1,0:T(8,128)(2,1)S(1)}, bf16[256,256]{1,0:T(8,128)(2,1)}, u32[]{:S(2)}) copy-start(bf16[256,256]{1,0:T(8,128)(2,1)} %param.38) | copy-start | bytes 393220
  709.6 29.2 %all-to-all-start.4 = ((bf16[128,32,256]{2,1,0:T(8,128)(2,1)}), bf16[128,32,256]{2,1,0:T(8,128)(2,1)S(1)}, u32[]{:S(2)}, u32[]{:S(2)}) async-start(bf16[128,32,256]{2,1,0:T(8,128)(2,1)} %copy.418), calls=%async_computation.7 | async-start | bytes 4194304 | tf_op jit(solution)/shard_map/all_to_all | solution.py:112
  713.4 111.2 %reduce-scatter.13.cloned.1.call-start = ((), (), s32[]{:S(2)}) async-start(), calls=%async_computation.17 | async-start | bytes 655360 | tf_op jit(solution)/shard_map/reduce_scatter | solution.py:104
  796.3 218.7 %reduce-scatter.15.cloned.1.call-start = ((), (), s32[]{:S(2)}) async-start(), calls=%async_computation.18 | async-start | bytes 20971520 | tf_op jit(solution)/shard_map/reduce_scatter | solution.py:104
  832.2 213.2 %copy-start.156 = (f32[32,128]{1,0:T(8,128)}, f32[32,128]{1,0:T(8,128)S(1)}, u32[]{:S(2)}) copy-start(f32[32,128]{1,0:T(8,128)S(1)} %multiply_multiply_fusion.5) | copy-start | bytes 49156
  834.8 210.6 %copy-start.183 = (f32[32,128]{1,0:T(8,128)}, f32[32,128]{1,0:T(8,128)S(1)}, u32[]{:S(2)}) copy-start(f32[32,128]{1,0:T(8,128)S(1)} %negate_multiply_fusion.4) | copy-start | bytes 49156
  893.7 41.8 %all-to-all-start.5 = ((bf16[128,32,256]{2,1,0:T(8,128)(2,1)}), bf16[128,32,256]{2,1,0:T(8,128)(2,1)}, u32[]{:S(2)}, u32[]{:S(2)}) async-start(bf16[128,32,256]{2,1,0:T(8,128)(2,1)} %copy.433), calls=%async_computation.10 | async-start | bytes 4194304 | tf_op jit(solution)/shard_map/all_to_all | solution.py:148
  898.2 233.9 %reduce-scatter.9.cloned.1.call-start = ((), (), s32[]{:S(2)}) async-start(), calls=%async_computation.15 | async-start | bytes 245760 | tf_op jit(solution)/shard_map/reduce_scatter | solution.py:104
  899.6 233.3 %reduce-scatter.7.cloned.1.call-start = ((), (), s32[]{:S(2)}) async-start(), calls=%async_computation.14 | async-start | bytes 245760 | tf_op jit(solution)/shard_map/reduce_scatter | solution.py:104
  900.8 317.9 %reduce-scatter.17.cloned.1.call-start = ((), (), s32[]{:S(2)}) async-start(), calls=%async_computation.19 | async-start | bytes 20971520 | tf_op jit(solution)/shard_map/reduce_scatter | solution.py:104
  939.9 91.0 %copy-start.103 = (f32[32,128]{1,0:T(8,128)S(1)}, f32[32,128]{1,0:T(8,128)}, u32[]{:S(2)}) copy-start(f32[32,128]{1,0:T(8,128)} %copy-done.102) | copy-start | bytes 49156
  939.9 91.0 %copy-start.137 = (bf16[256,1024]{1,0:T(8,128)(2,1)S(1)}, bf16[256,1024]{1,0:T(8,128)(2,1)}, u32[]{:S(2)}) copy-start(bf16[256,1024]{1,0:T(8,128)(2,1)} %param.33) | copy-start | bytes 1572868
  1094.3 1029.3 %all-reduce.28.cloned.1.call-start = ((), (), s32[]{:S(2)}) async-start(), calls=%async_computation.20 | async-start | bytes 4751360 | tf_op jit(solution)/shard_map/psum | solution.py:214
  1267.9 47.2 %copy-start.74 = (bf16[589824]{0:T(1024)(128)(2,1)S(1)}, bf16[589824]{0:T(1024)(128)(2,1)}, u32[]{:S(2)}) copy-start(bf16[589824]{0:T(1024)(128)(2,1)} %reshape.539) | copy-start | bytes 3538948
  2069.2 57.7 %copy-start.1 = (bf16[384,3072]{1,0:T(8,128)(2,1)S(1)}, bf16[384,3072]{1,0:T(8,128)(2,1)}, u32[]{:S(2)}) copy-start(bf16[384,3072]{1,0:T(8,128)(2,1)} %param.48) | copy-start | bytes 7077892
  (230 other events, 1478.8 us)
Sparse Core Ops, SparseCore 0:
  21.9 61.2 all-gather.2
  124.5 80.5 all-gather.4
  661.5 21.5 reduce-scatter.10
  796.4 21.5 reduce-scatter.12
  878.9 136.0 reduce-scatter.14
  1017.3 19.7 reduce-scatter.8
  1039.5 19.7 reduce-scatter.6
  1094.4 124.3 reduce-scatter.16
  2069.2 54.3 all-reduce.27
where the time goes:
time: 2150 us; the launch traced here: 2130 us
  blocking collectives  798 us (37%)
  matrix products  427 us (20%)
  local copies, waits for them, and re-layouts  335 us (16%)
  waiting for transfers between devices  321 us (15%)
  other arithmetic  213 us (10%)
  starting transfers between devices  22 us (1%)
    unnamed x1, blocking collectives  731 us
    unnamed x531, local copies, waits for them, and re-layouts  104 us
    reduce_scatter x6, waiting for transfers between devices, scatter_rows(): return lax.psum_scatter(x_in, GROUP_AXIS, scatter_dimension=0, tiled=True)  79.3 us
    all_gather x2, waiting for transfers between devices, gather_rows(): return lax.all_gather(x_in, GROUP_AXIS, axis=0, tiled=True)  71.2 us
    dot_general x6, matrix products, att_core(): jnp.einsum('ihjk,ikhd->ijhd', prob_mat, v_rows, preferred_element_type=jn...  53.9 us
    all_to_all x1, waiting for transfers between devices, mul_in_forward(): left_cols = lax.all_to_all(left_proj, GROUP_AXIS, 1, 0, tiled=True)  47.8 us
    dot_general x6, matrix products, att_pre(): proj_all = jnp.dot(normed, w_qkvg, preferred_element_type=jnp.float32)  44.9 us
    psum x1, waiting for transfers between devices, device_step(): grad_flat = lax.psum(grad_flat, GROUP_AXIS)  43.9 us
  transfers between devices with their start and end apart: 14, of which 9 were waited for; matrix products, arithmetic and copies ran while one was open for 15% of the time, Pallas kernels for 0%

commit v1 on v0

v1 whole, which is shorter than its diff:
```python
import functools
import jax
import jax.numpy as jnp
from jax import lax
from jax.experimental import pallas as pl
from jax.experimental.pallas import tpu as pltpu
from jax.sharding import PartitionSpec as P


BATCH_AXIS = 'dp'
GROUP_AXIS = 'dap'
MASK_PENALTY = 1.0e9
NCH = 4
WORK = 1 << 12

NORM_EPS = 1e-5
F32 = jnp.float32
BF16 = jnp.bfloat16


def mm(a, b):
    return lax.dot_general(a, b, (((1,), (0,)), ((), ())), preferred_element_type=F32)


def mm_nt(a, b):
    return lax.dot_general(a, b, (((1,), (1,)), ((), ())), preferred_element_type=F32)


def mm_tn(a, b):
    return lax.dot_general(a, b, (((0,), (0,)), ((), ())), preferred_element_type=F32)


def ln_stats(x):
    inv = 1.0 / x.shape[-1]
    c = x - jnp.sum(x, axis=-1, keepdims=True) * inv
    r = lax.rsqrt(jnp.sum(c * c, axis=-1, keepdims=True) * inv + NORM_EPS)
    return c * r, r


def ln_back(dn, xh, r):
    inv = 1.0 / dn.shape[-1]
    m1 = jnp.sum(dn, axis=-1, keepdims=True) * inv
    m2 = jnp.sum(dn * xh, axis=-1, keepdims=True) * inv
    return r * (dn - m1 - xh * m2)


def put_flat(ref, val):
    n = val.shape[1] // 128
    for t in range(n):
        ref[pl.ds(t, val.shape[0], stride=n), :] = val[:, t * 128:(t + 1) * 128]


def flat_shape(w):
    return jax.ShapeDtypeStruct((w.size // 128, 128), F32)


def last_step():
    return pl.program_id(0) == pl.num_programs(0) - 1


def sig(x):
    return 1.0 / (1.0 + jnp.exp(-x))


def trans_fwd_body(z_ref, wu_ref, wd_ref, o_ref):
    x = z_ref[...].astype(F32)
    xh, _ = ln_stats(x)
    h = mm(xh.astype(BF16), wu_ref[...])
    d = h.shape[1] // 2
    h1 = h[:, :d]
    act = (h1 * sig(h1) * h[:, d:]).astype(BF16)
    o_ref[...] = (x + mm(act, wd_ref[...])).astype(BF16)


def trans_bwd_body(z_ref, g_ref, wu_ref, wd_ref, dz_ref, fu_ref, fd_ref, dwu_ref, dwd_ref):
    @pl.when(pl.program_id(0) == 0)
    def _():
        dwu_ref[...] = jnp.zeros_like(dwu_ref)
        dwd_ref[...] = jnp.zeros_like(dwd_ref)

    x = z_ref[...].astype(F32)
    xh, r = ln_stats(x)
    n = xh.astype(BF16)
    h = mm(n, wu_ref[...])
    d = h.shape[1] // 2
    h1, h2 = h[:, :d], h[:, d:]
    s = sig(h1)
    sl = h1 * s
    act = (sl * h2).astype(BF16)
    g = g_ref[...]
    da = mm_nt(g, wd_ref[...]).astype(BF16).astype(F32)
    dwd_ref[...] += mm_tn(act, g)
    dh1 = (da * h2 * (s + sl * (1.0 - s))).astype(BF16)
    dh2 = (da * sl).astype(BF16)
    dh = jnp.concatenate([dh1, dh2], axis=1)
    dwu_ref[...] += mm_tn(n, dh)
    dn = mm_nt(dh, wu_ref[...])
    dz_ref[...] = (g.astype(F32) + ln_back(dn, xh, r)).astype(BF16)

    @pl.when(last_step())
    def _():
        put_flat(fu_ref, dwu_ref[...])
        put_flat(fd_ref, dwd_ref[...])


def row_spec(b):
    return pl.BlockSpec((b, T, C), lambda i: (i, 0, 0))


def full(a):
    nd = len(a.shape)
    return pl.BlockSpec(a.shape, lambda i: (0,) * nd)


def cp(flops):
    return dict(cost_estimate=pl.CostEstimate(flops=flops, bytes_accessed=1 << 23, transcendentals=0),
                compiler_params=pltpu.CompilerParams(vmem_limit_bytes=60 << 20, dimension_semantics=("arbitrary",)))


def trans_fwd(z, wu, wd, blk):
    p, c = z.shape
    spec = pl.BlockSpec((blk, c), lambda i: (i, 0))
    return pl.pallas_call(trans_fwd_body, grid=(p // blk,), in_specs=[spec, full(wu), full(wd)], out_specs=spec,
                          out_shape=jax.ShapeDtypeStruct((p, c), BF16), name="trans_fwd", **cp(p * c * WORK))(z, wu, wd)


def trans_bwd(z, g, wu, wd, blk):
    p, c = z.shape
    spec = pl.BlockSpec((blk, c), lambda i: (i, 0))
    return pl.pallas_call(trans_bwd_body, grid=(p // blk,), in_specs=[spec, spec, full(wu), full(wd)],
                          out_specs=[spec, full(flat_shape(wu)), full(flat_shape(wd))],
                          out_shape=[jax.ShapeDtypeStruct((p, c), BF16), flat_shape(wu), flat_shape(wd)],
                          scratch_shapes=[pltpu.VMEM(wu.shape, F32), pltpu.VMEM(wd.shape, F32)],
                          name="trans_bwd", **cp(p * c * WORK))(z, g, wu, wd)


H = 8
D = 32
T = 128
C = 256


def head_masks(width, dim):
    lane = lax.broadcasted_iota(jnp.int32, (1, width), 1)
    return [((lane >= h * dim) & (lane < (h + 1) * dim)).astype(F32).astype(BF16) for h in range(width // dim)]


def pair_setup():
    masks = head_masks(C, D)
    n = H // 2
    lane = lax.broadcasted_iota(jnp.int32, (1, C), 1)
    low = (lane < T).astype(F32).astype(BF16)
    return [a + b for a, b in zip(masks[:n], masks[n:])], [low, 1 - low]


def row_masks():
    row = lax.broadcasted_iota(jnp.int32, (C, 1), 0) // D % (H // 2)
    return [(row == m).astype(F32).astype(BF16) for m in range(H // 2)]


def unpair(x, pairs):
    return sum(x[m * T:(m + 1) * T] * p.astype(F32) for m, p in enumerate(pairs))


def head_tn(x, w, flips):
    xt = x.astype(F32).T.astype(BF16)
    y = mm(jnp.concatenate([xt * f for f in flips], axis=1), w)
    return jnp.concatenate([y[:T, :T], y[T:, T:]]).T.astype(BF16)


def softmax(s):
    e = jnp.exp(s - jnp.max(s, axis=-1, keepdims=True))
    return e * (1.0 / jnp.sum(e, axis=-1, keepdims=True))


def stack_heads(x, masks):
    return jnp.concatenate([x * m for m in masks])


def bias_body(z_ref, wbt_ref, o_ref):
    for i in range(z_ref.shape[0]):
        xh, _ = ln_stats(z_ref[i].astype(F32))
        o_ref[i] = mm_nt(wbt_ref[...], xh.astype(BF16)).astype(BF16)


def att_bias(z3, wbt):
    r, h = z3.shape[0], wbt.shape[0]
    return pl.pallas_call(bias_body, grid=(r // 8,), in_specs=[row_spec(8), full(wbt)],
                          out_specs=pl.BlockSpec((8, h, T), lambda i: (i, 0, 0)),
                          out_shape=jax.ShapeDtypeStruct((r, h, T), BF16), name="att_bias", **cp(r * T * C * WORK))(z3, wbt)


def att_fwd_body(z_ref, bias_ref, wq_ref, wo_ref, o_ref):
    b = z_ref.shape[0]
    pairs, sides = pair_setup()
    x = z_ref[...].reshape(b * T, C).astype(F32)
    xh, _ = ln_stats(x)
    pr = mm(xh.astype(BF16), wq_ref[...])
    gates = sig(pr[:, 3 * C:])
    prb = pr[:, :3 * C].astype(BF16)
    outs = []
    for i in range(b):
        row = prb[i * T:(i + 1) * T]
        q, k, v = row[:, :C], row[:, C:2 * C], row[:, 2 * C:]
        lg = mm_nt(stack_heads(q, pairs), stack_heads(k, sides)) * (D ** -0.5)
        ps = []
        for m in range(len(pairs)):
            s = lg[m * T:(m + 1) * T]
            ps.append(jnp.concatenate([softmax(s[:, :T] + bias_ref[m]), softmax(s[:, T:] + bias_ref[m + len(pairs)])], axis=1).astype(BF16))
        o = unpair(mm(jnp.concatenate(ps), stack_heads(v, sides)), pairs)
        outs.append((gates[i * T:(i + 1) * T] * o).astype(BF16))
    gated = jnp.concatenate(outs)
    o_ref[...] = (x + mm(gated, wo_ref[...])).astype(BF16).reshape(b, T, C)


def att_fwd(z3, bias, wq, wo, b):
    r = z3.shape[0]
    spec = row_spec(b)
    return pl.pallas_call(att_fwd_body, grid=(r // b,), in_specs=[spec, full(bias), full(wq), full(wo)], out_specs=spec,
                          out_shape=jax.ShapeDtypeStruct((r, T, C), BF16), name="att_fwd",
                          **cp(r * T * C * WORK))(z3, bias, wq, wo)


def att_bwd_body(z_ref, g_ref, bias_ref, wq_ref, wo_ref, dn_ref, dbias_ref, fq_ref, fo_ref, dwq_ref, dwo_ref):
    @pl.when(pl.program_id(0) == 0)
    def _():
        dbias_ref[...] = jnp.zeros_like(dbias_ref)
        dwq_ref[...] = jnp.zeros_like(dwq_ref)
        dwo_ref[...] = jnp.zeros_like(dwo_ref)

    b = z_ref.shape[0]
    pairs, sides = pair_setup()
    flips = row_masks()
    x = z_ref[...].reshape(b * T, C).astype(F32)
    g = g_ref[...].reshape(b * T, C)
    xh, _ = ln_stats(x)
    n = xh.astype(BF16)
    pr = mm(n, wq_ref[...])
    gates = sig(pr[:, 3 * C:])
    prb = pr[:, :3 * C].astype(BF16)
    dgd = mm_nt(g, wo_ref[...]).astype(BF16).astype(F32)
    do_all = (dgd * gates).astype(BF16)
    gat, dps = [], []
    for i in range(b):
        sl = slice(i * T, (i + 1) * T)
        row = prb[sl]
        q, k, v = row[:, :C], row[:, C:2 * C], row[:, 2 * C:]
        do = do_all[sl]
        qs, dos = stack_heads(q, pairs), stack_heads(do, pairs)
        kk, vv = stack_heads(k, sides), stack_heads(v, sides)
        lg = mm_nt(qs, kk) * (D ** -0.5)
        dp = mm_nt(dos, vv)
        ps, ds = [], []
        for m in range(len(pairs)):
            pp, dd = [], []
            for e in range(2):
                h = m + e * len(pairs)
                blk = (slice(m * T, (m + 1) * T), slice(e * T, (e + 1) * T))
                p = softmax(lg[blk] + bias_ref[h])
                pd = p * dp[blk].astype(BF16).astype(F32)
                dsh = pd - p * jnp.sum(pd, axis=-1, keepdims=True)
                dbias_ref[h] += dsh
                pp.append(p.astype(BF16))
                dd.append((dsh * (D ** -0.5)).astype(BF16))
            ps.append(jnp.concatenate(pp, axis=1))
            ds.append(jnp.concatenate(dd, axis=1))
        ps, ds = jnp.concatenate(ps), jnp.concatenate(ds)
        o = unpair(mm(ps, vv), pairs)
        dq = unpair(mm(ds, kk), pairs).astype(BF16)
        dk, dv = head_tn(q, ds, flips), head_tn(do, ps, flips)
        gt = gates[sl]
        gat.append((gt * o).astype(BF16))
        dgl = (dgd[sl] * o * gt * (1.0 - gt)).astype(BF16)
        dps.append(jnp.concatenate([dq, dk, dv, dgl], axis=1))
    gated = jnp.concatenate(gat)
    dpr = jnp.concatenate(dps)
    dwo_ref[...] += mm_tn(gated, g)
    dwq_ref[...] += mm_tn(n, dpr)
    dn_ref[...] = mm_nt(dpr, wq_ref[...])

    @pl.when(last_step())
    def _():
        put_flat(fq_ref, dwq_ref[...])
        put_flat(fo_ref, dwo_ref[...])


def att_bwd(z3, g3, bias, wq, wo, b):
    r = z3.shape[0]
    spec = row_spec(b)
    return pl.pallas_call(att_bwd_body, grid=(r // b,), in_specs=[spec, spec, full(bias), full(wq), full(wo)],
                          out_specs=[pl.BlockSpec((b * T, C), lambda i: (i, 0)), full(bias), full(flat_shape(wq)), full(flat_shape(wo))],
                          out_shape=[jax.ShapeDtypeStruct((r * T, C), F32), jax.ShapeDtypeStruct(bias.shape, F32), flat_shape(wq), flat_shape(wo)],
                          scratch_shapes=[pltpu.VMEM(wq.shape, F32), pltpu.VMEM(wo.shape, F32)],
                          name="att_bwd", **cp(r * T * C * WORK))(z3, g3, bias, wq, wo)


def att_fin_body(z_ref, g_ref, db_ref, wbt_ref, *rest):
    dz_ref, dwbt_ref = rest[-2:]

    @pl.when(pl.program_id(0) == 0)
    def _():
        dwbt_ref[...] = jnp.zeros_like(dwbt_ref)

    b = z_ref.shape[0]
    xh, r = ln_stats(z_ref[...].reshape(b * T, C).astype(F32))
    n = xh.astype(BF16)
    parts = []
    for i in range(b):
        db = db_ref[i].astype(BF16)
        parts.append(mm_tn(db, wbt_ref[...]))
        dwbt_ref[...] += mm(db, n[i * T:(i + 1) * T])
    dn = jnp.concatenate(parts)
    if len(rest) == 3:
        dn = dn + rest[0][...]
    dz_ref[...] = (g_ref[...].reshape(b * T, C).astype(F32) + ln_back(dn, xh, r)).astype(BF16).reshape(b, T, C)


def att_fin(z3, g3, db, wbt, dn=None):
    r, h = z3.shape[0], wbt.shape[0]
    b = 8
    spec = row_spec(b)
    extra = [] if dn is None else [dn]
    return pl.pallas_call(att_fin_body, grid=(r // b,),
                          in_specs=[spec, spec, pl.BlockSpec((b, h, T), lambda i: (i, 0, 0)), full(wbt)]
                          + [pl.BlockSpec((b * T, C), lambda i: (i, 0))] * len(extra),
                          out_specs=[spec, full(wbt)],
                          out_shape=[jax.ShapeDtypeStruct((r, T, C), BF16), jax.ShapeDtypeStruct(wbt.shape, F32)],
                          name="att_fin", **cp(r * T * C * WORK))(z3, g3, db, wbt, *extra)


RB = 16
CB = 32


def put_row(scr, i, val):
    scr[pl.ds(i, val.shape[0], stride=RB), :] = val


def get_row(scr, i, n):
    return scr[pl.ds(i, n, stride=RB), :]


def cspecs(n):
    return [pl.BlockSpec((C // n, RB, T), lambda i: (0, i, 0))] * n


def cshapes(n, r, dt=BF16):
    return [jax.ShapeDtypeStruct((C // n, r, T), dt)] * n


def flush(scr, refs):
    w = C // len(refs)
    for p, ref in enumerate(refs):
        ref[...] = scr[pl.ds(p * w * RB, w * RB), :].reshape(w, RB, T).astype(BF16)


def mul_pre_body(z_ref, wt_ref, *rest):
    outs, sa, sb = rest[:-2], rest[-2], rest[-1]
    wt = wt_ref[...]
    for i in range(0, RB, 2):
        xh, _ = ln_stats(z_ref[i:i + 2].reshape(2 * T, C).astype(F32))
        pt = mm_nt(wt, xh.astype(BF16))
        at = sig(pt[C:2 * C]) * pt[:C]
        bt = sig(pt[3 * C:]) * pt[2 * C:3 * C]
        for e in range(2):
            put_row(sa, i + e, at[:, e * T:(e + 1) * T])
            put_row(sb, i + e, bt[:, e * T:(e + 1) * T])
    flush(sa, outs[:NCH])
    flush(sb, outs[NCH:])


def mul_pre(z3, wt):
    r = z3.shape[0]
    zs = row_spec(RB)
    out = pl.pallas_call(mul_pre_body, grid=(r // RB,), in_specs=[zs, full(wt)], out_specs=cspecs(NCH) * 2, out_shape=cshapes(NCH, r) * 2,
                         scratch_shapes=[pltpu.VMEM((C * RB, T), F32)] * 2, name="mul_pre", **cp(r * T * C * WORK))(z3, wt)
    return out[:NCH], out[NCH:]


def collect(idx_ref, refs, buf):
    for rel, ref in enumerate(refs):
        r = ref.shape[1]
        buf[:, pl.ds(pl.multiple_of(idx_ref[rel] * r, r), r), :] = ref[...]


def mix_call(body, idx, ins, n_out, out_dt, n_buf):
    w, r, _ = ins[0].shape
    spec = pl.BlockSpec((CB, r, T), lambda i, s: (i, 0, 0))
    gs = pltpu.PrefetchScalarGridSpec(num_scalar_prefetch=1, grid=(w // CB,), in_specs=[spec] * len(ins), out_specs=[spec] * n_out,
                                      scratch_shapes=[pltpu.VMEM((CB, T, T), BF16)] * n_buf)
    return pl.pallas_call(body, grid_spec=gs, out_shape=[jax.ShapeDtypeStruct((w, r, T), out_dt)] * n_out, **cp(r * w * T * WORK))(idx, *ins)


def mix_fwd_body(idx_ref, a_ref, b0, b1, b2, b3, x_ref, buf):
    collect(idx_ref, (b0, b1, b2, b3), buf)
    for c in range(CB):
        x_ref[c] = mm_nt(a_ref[c], buf[c])


def mix_fwd(idx, a, b4):
    return mix_call(mix_fwd_body, idx, [a, *b4], 1, F32, 1)[0]


def mix_bwd_out_body(idx_ref, dx_ref, dt_ref, b0, b1, b2, b3, a0, a1, a2, a3, da_ref, db_ref, bb, ab):
    collect(idx_ref, (b0, b1, b2, b3), bb)
    collect(idx_ref, (a0, a1, a2, a3), ab)
    for c in range(CB):
        da_ref[c] = mm(dx_ref[c], bb[c]).astype(BF16)
        db_ref[c] = mm(dt_ref[c], ab[c]).astype(BF16)


def mix_bwd_out(idx, dx, dxt, b4, a4):
    return mix_call(mix_bwd_out_body, idx, [dx, dxt, *b4, *a4], 2, BF16, 2)


def mix_bwd_in_body(idx_ref, a_ref, b_ref, d0, d1, d2, d3, da_ref, db_ref, buf):
    collect(idx_ref, (d0, d1, d2, d3), buf)
    for c in range(CB):
        d = buf[c]
        da_ref[c] = mm_nt(b_ref[c], d).astype(BF16)
        db_ref[c] = mm(a_ref[c], d).astype(BF16)


def mix_bwd_in(idx, d4, a, b):
    return mix_call(mix_bwd_in_body, idx, [a, b, *d4], 2, BF16, 1)


def ln0_stats(x):
    inv = 1.0 / x.shape[0]
    c = x - jnp.sum(x, axis=0, keepdims=True) * inv
    r = lax.rsqrt(jnp.sum(c * c, axis=0, keepdims=True) * inv + NORM_EPS)
    return c * r, r


def ln0_back(dn, xh, r):
    inv = 1.0 / dn.shape[0]
    m1 = jnp.sum(dn, axis=0, keepdims=True) * inv
    m2 = jnp.sum(dn * xh, axis=0, keepdims=True) * inv
    return r * (dn - m1 - xh * m2)


def col_of(refs, i):
    return jnp.concatenate([ref[:, i, :] for ref in refs])


def mul_post_body(*refs):
    xs, (z_ref, wg_ref, wo_ref, o_ref) = refs[:NCH], refs[NCH:]
    for i in range(z_ref.shape[0]):
        z = z_ref[i].astype(F32)
        n, _ = ln_stats(z)
        g = sig(mm(n.astype(BF16), wg_ref[...]))
        xn, _ = ln0_stats(col_of(xs, i))
        o_ref[i] = (z + g * mm_tn(xn.astype(BF16), wo_ref[...])).astype(BF16)


def mul_post(xs, z3, wg, wo):
    r = z3.shape[0]
    b = 8
    zs = row_spec(b)
    xspec = pl.BlockSpec((C // NCH, b, T), lambda i: (0, i, 0))
    return pl.pallas_call(mul_post_body, grid=(r // b,), in_specs=[xspec] * NCH + [zs, full(wg), full(wo)],
                          out_specs=zs, out_shape=jax.ShapeDtypeStruct((r, T, C), BF16), name="mul_post", **cp(r * T * C * WORK))(*xs, z3, wg, wo)


def mul_post_bwd_body(pix, *refs):
    xs, (z_ref, d_ref, wg_ref, wo_ref) = refs[:NCH], refs[NCH:NCH + 4]
    dxs, (dgl_ref, fo_ref) = refs[NCH + 4:2 * NCH + 4], refs[2 * NCH + 4:2 * NCH + 6]
    scr, dwo_ref = refs[-2:]

    @pl.when(pl.program_id(0) == 0)
    def _():
        dwo_ref[...] = jnp.zeros_like(dwo_ref)

    for i in range(RB):
        n, _ = ln_stats(z_ref[i].astype(F32))
        g = sig(mm(n.astype(BF16), wg_ref[...]))
        xh, r = ln0_stats(col_of(xs, i))
        xn = xh.astype(BF16)
        u = mm_tn(xn, wo_ref[...])
        d = d_ref[i].astype(F32)
        du = (d * g).astype(BF16)
        dgl_ref[i] = (d * u * g * (1.0 - g)).astype(BF16)
        dwo_ref[...] += mm(xn, du)
        dx = ln0_back(mm_nt(wo_ref[...], du), xh, r)
        put_row(scr, i, dx)
        if pix:
            refs[2 * NCH + 6][i] = dx.T.astype(BF16)
    flush(scr, dxs)

    @pl.when(last_step())
    def _():
        put_flat(fo_ref, dwo_ref[...])


def mul_post_bwd(xs, z3, d3, wg, wo, pix):
    r = z3.shape[0]
    zs = row_spec(RB)
    zsh = jax.ShapeDtypeStruct((r, T, C), BF16)
    out = pl.pallas_call(functools.partial(mul_post_bwd_body, pix), grid=(r // RB,), in_specs=cspecs(NCH) + [zs, zs, full(wg), full(wo)],
                         out_specs=cspecs(NCH) + [zs, full(flat_shape(wo))] + [zs] * pix,
                         out_shape=cshapes(NCH, r) + [zsh, flat_shape(wo)] + [zsh] * pix,
                         scratch_shapes=[pltpu.VMEM((C * RB, T), F32), pltpu.VMEM(wo.shape, F32)],
                         name="mul_post_bwd", **cp(r * T * C * WORK))(*xs, z3, d3, wg, wo)
    return (out[:NCH], *out[NCH:])


def flip_body(d_ref, *rest):
    sin, sout = rest[-2:]
    for hf in range(2):
        sin[hf] = d_ref[:, :, hf * T:(hf + 1) * T].astype(F32).reshape(T * RB, T)
    for j in range(RB):
        for hf in range(2):
            m = sin[hf, pl.ds(j, T, stride=RB), :]
            sout[pl.ds(hf * T * RB + j, T, stride=RB), :] = m.T
    flush(sout, rest[:-2])


def flip(d):
    r = d.shape[1]
    return pl.pallas_call(flip_body, grid=(r // RB,), in_specs=[pl.BlockSpec((T, RB, C), lambda i: (0, i, 0))],
                          out_specs=cspecs(NCH), out_shape=cshapes(NCH, r),
                          scratch_shapes=[pltpu.VMEM((2, T * RB, T), F32), pltpu.VMEM((C * RB, T), F32)], name="flip", **cp(r * T * C * WORK))(d)


def load_all(scr, refs):
    w = C // len(refs)
    for p, ref in enumerate(refs):
        scr[pl.ds(p * w * RB, w * RB), :] = ref[...].astype(F32).reshape(w * RB, T)


def mul_pre_bwd_body(*refs):
    das, dbs = refs[:NCH], refs[NCH:2 * NCH]
    z_ref, g_ref, dgl_ref, w_ref, wt_ref, wg_ref, dz_ref, fi_ref, fg_ref, sa, sb, dwt_ref, dwg_ref = refs[2 * NCH:]

    @pl.when(pl.program_id(0) == 0)
    def _():
        dwt_ref[...] = jnp.zeros_like(dwt_ref)
        dwg_ref[...] = jnp.zeros_like(dwg_ref)

    load_all(sa, das)
    load_all(sb, dbs)
    for i in range(0, RB, 2):
        xh, r = ln_stats(z_ref[i:i + 2].reshape(2 * T, C).astype(F32))
        n = xh.astype(BF16)
        pt = mm_nt(wt_ref[...], n)
        da = jnp.concatenate([get_row(sa, i, C), get_row(sa, i + 1, C)], axis=1)
        db = jnp.concatenate([get_row(sb, i, C), get_row(sb, i + 1, C)], axis=1)
        s1, s2 = sig(pt[C:2 * C]), sig(pt[3 * C:])
        d1, d3 = da * s1, db * s2
        dp = jnp.concatenate([d1.astype(BF16), (d1 * pt[:C] * (1.0 - s1)).astype(BF16),
                              d3.astype(BF16), (d3 * pt[2 * C:3 * C] * (1.0 - s2)).astype(BF16)])
        dgl = dgl_ref[i:i + 2].reshape(2 * T, C)
        dwt_ref[...] += mm(dp, n)
        dwg_ref[...] += mm_tn(n, dgl)
        dn = mm(w_ref[...], dp).T + mm_nt(dgl, wg_ref[...])
        dz = g_ref[i:i + 2].reshape(2 * T, C).astype(F32) + ln_back(dn, xh, r)
        dz_ref[i:i + 2] = dz.astype(BF16).reshape(2, T, C)

    @pl.when(last_step())
    def _():
        put_flat(fi_ref, dwt_ref[...].T)
        put_flat(fg_ref, dwg_ref[...])


def mul_pre_bwd(z3, g3, das, dbs, dgl, w, wt, wg):
    r = z3.shape[0]
    zs = row_spec(RB)
    return pl.pallas_call(mul_pre_bwd_body, grid=(r // RB,), in_specs=cspecs(NCH) * 2 + [zs, zs, zs, full(w), full(wt), full(wg)],
                          out_specs=[zs, full(flat_shape(wt)), full(flat_shape(wg))],
                          out_shape=[jax.ShapeDtypeStruct((r, T, C), BF16), flat_shape(wt), flat_shape(wg)],
                          scratch_shapes=[pltpu.VMEM((C * RB, T), F32)] * 2 + [pltpu.VMEM(wt.shape, F32), pltpu.VMEM(wg.shape, F32)],
                          name="mul_pre_bwd", **cp(r * T * C * WORK))(*das, *dbs, z3, g3, dgl, w, wt, wg)


SH = 16
SD = 24


def single_body(s_ref, d_ref, bias_ref, wq_ref, qb_ref, wo_ref, wu_ref, wd_ref,
                so_ref, ds_ref, dbias_ref, dqb_ref, dwq_ref, dwo_ref, dwu_ref, dwd_ref):
    w = s_ref.shape[1]
    masks = head_masks(w, SD)
    x = s_ref[...].astype(F32)
    xh, r = ln_stats(x)
    n = xh.astype(BF16)
    pr = mm(n, wq_ref[...])
    q = (pr[:, :w] + qb_ref[...].astype(F32)).astype(BF16)
    k = pr[:, w:2 * w].astype(BF16)
    v = pr[:, 2 * w:3 * w].astype(BF16)
    gt = sig(pr[:, 3 * w:])
    qs = stack_heads(q, masks)
    lg = mm_nt(qs, k) * (SD ** -0.5)
    pf, ps = [], []
    for h in range(SH):
        p = softmax(lg[h * T:(h + 1) * T] + bias_ref[h].T)
        pf.append(p)
        ps.append(p.astype(BF16))
    o = mm(jnp.concatenate(ps, axis=1), stack_heads(v, masks))
    gated = (gt * o).astype(BF16)
    s1 = (x + mm(gated, wo_ref[...])).astype(BF16)
    x1 = s1.astype(F32)
    xh1, r1 = ln_stats(x1)
    n1 = xh1.astype(BF16)
    hid = mm(n1, wu_ref[...])
    d = hid.shape[1] // 2
    h1, h2 = hid[:, :d], hid[:, d:]
    sg = sig(h1)
    sl = h1 * sg
    act = (sl * h2).astype(BF16)
    so_ref[...] = (x1 + mm(act, wd_ref[...])).astype(BF16)
    g = d_ref[...]
    da = mm_nt(g, wd_ref[...]).astype(BF16).astype(F32)
    put_flat(dwd_ref, mm_tn(act, g))
    dh = jnp.concatenate([(da * h2 * (sg + sl * (1.0 - sg))).astype(BF16), (da * sl).astype(BF16)], axis=1)
    put_flat(dwu_ref, mm_tn(n1, dh))
    g1 = (g.astype(F32) + ln_back(mm_nt(dh, wu_ref[...]), xh1, r1)).astype(BF16)
    dgd = mm_nt(g1, wo_ref[...]).astype(BF16).astype(F32)
    put_flat(dwo_ref, mm_tn(gated, g1))
    do = (dgd * gt).astype(BF16)
    dgl = (dgd * o * gt * (1.0 - gt)).astype(BF16)
    dos = stack_heads(do, masks)
    dp = mm_nt(dos, v)
    ds = []
    for h in range(SH):
        pd = pf[h] * dp[h * T:(h + 1) * T].astype(BF16).astype(F32)
        dsh = pd - pf[h] * jnp.sum(pd, axis=-1, keepdims=True)
        dbias_ref[h] = dsh.T
        ds.append((dsh * (SD ** -0.5)).astype(BF16))
    dq = mm(jnp.concatenate(ds, axis=1), stack_heads(k, masks)).astype(BF16)
    dk = mm_tn(jnp.concatenate(ds), qs).astype(BF16)
    dv = mm_tn(jnp.concatenate(ps), dos).astype(BF16)
    dqb_ref[...] = jnp.sum(dq.astype(F32), axis=0, keepdims=True)
    dpr = jnp.concatenate([dq, dk, dv, dgl], axis=1)
    put_flat(dwq_ref, mm_tn(n, dpr))
    ds_ref[...] = (g1.astype(F32) + ln_back(mm_nt(dpr, wq_ref[...]), xh, r)).astype(BF16)


def single_step(s, d, bias, wq, qb, wo, wu, wd):
    vm = pl.BlockSpec(memory_space=pltpu.VMEM)
    sh = [jax.ShapeDtypeStruct(s.shape, BF16)] * 2 + [jax.ShapeDtypeStruct(a.shape, F32) for a in (bias, qb)] + [flat_shape(a) for a in (wq, wo, wu, wd)]
    return pl.pallas_call(single_body, in_specs=[vm] * 8, out_specs=[vm] * 8, out_shape=sh, name="single_step",
                          cost_estimate=pl.CostEstimate(flops=1 << 33, bytes_accessed=1 << 24, transcendentals=0),
                          compiler_params=pltpu.CompilerParams(vmem_limit_bytes=60 << 20))(s, d, bias, wq, qb, wo, wu, wd)


def flip_perm(bit):
    return [(i, i ^ bit) for i in range(4)]


def swap_core(x_in):
    return lax.ppermute(x_in, GROUP_AXIS, flip_perm(1))


def swap_chip(x_in):
    return lax.ppermute(x_in, GROUP_AXIS, flip_perm(2))


def gather_rel(xs):
    out = []
    for x_in in xs:
        near = swap_core(x_in)
        far = swap_chip(x_in)
        out.append((x_in, near, far, swap_core(far)))
    return out


def mix_all(fn, *chunks):
    out = []
    for args in zip(*chunks):
        out.append(fn(*args))
    return out


def rows_to_cols(x_in):
    return jnp.transpose(lax.all_to_all(x_in, GROUP_AXIS, 1, 0, tiled=True), (1, 0, 2))


def cols_to_rows(x_in):
    return lax.all_to_all(jnp.transpose(x_in, (1, 0, 2)), GROUP_AXIS, 0, 1, tiled=True)


def scatter_rows(x_in):
    me = lax.axis_index(GROUP_AXIS)
    chip, core = me // 2, me % 2
    halves = x_in.reshape((2, 2) + (x_in.shape[0] // 4,) + x_in.shape[1:])
    mine = lax.dynamic_index_in_dim(halves, chip, 0, keepdims=False)
    mine = mine + swap_chip(lax.dynamic_index_in_dim(halves, 1 - chip, 0, keepdims=False))
    own = lax.dynamic_index_in_dim(mine, core, 0, keepdims=False)
    return own + swap_core(lax.dynamic_index_in_dim(mine, 1 - core, 0, keepdims=False))


def bias_full(part, mask_add):
    return jnp.transpose(lax.all_gather(part, GROUP_AXIS, axis=0, tiled=True), (1, 0, 2)).astype(F32) + mask_add


def group_half(pieces, partial):
    core = lax.axis_index(GROUP_AXIS) % 2
    rows = sum(p.shape[0] for p in pieces)
    pad = -rows % 128
    flat = jnp.concatenate(list(pieces) + ([jnp.zeros((pad, 128), F32)] if pad else []), axis=0)
    half = flat.shape[0] // 2
    mine = lax.dynamic_slice_in_dim(flat, core * half, half)
    if partial:
        mine = mine + swap_core(lax.dynamic_slice_in_dim(flat, (1 - core) * half, half))
    return mine


def scatter_group(mine):
    return lax.psum_scatter(mine, BATCH_AXIS, scatter_dimension=0, tiled=True)


def gather_group(part, partial):
    if partial:
        part = part + swap_chip(part)
    got = lax.all_gather(part, BATCH_AXIS, axis=0, tiled=True)
    return got, swap_core(got)


def dp_perm(bit):
    n = lax.axis_size(BATCH_AXIS)
    return [(i, i ^ bit) for i in range(n)]


def small_group(mine):
    me = lax.axis_index(BATCH_AXIS)
    bits = (1, 2, 4)
    for bit in bits:
        half = mine.shape[0] // 2
        side = (me // bit) % 2
        other = lax.ppermute(lax.dynamic_slice_in_dim(mine, (1 - side) * half, half), BATCH_AXIS, dp_perm(bit))
        mine = lax.dynamic_slice_in_dim(mine, side * half, half) + other
    mine = mine + swap_chip(mine)
    for bit in reversed(bits):
        half = mine.shape[0]
        side = (me // bit) % 2
        other = lax.ppermute(mine, BATCH_AXIS, dp_perm(bit))
        both = jnp.zeros((2 * half, 128), F32)
        both = lax.dynamic_update_slice_in_dim(both, mine, side * half, 0)
        mine = lax.dynamic_update_slice_in_dim(both, other, (1 - side) * half, 0)
    return mine, swap_core(mine)


def chunk_pieces(table, start, size, core):
    at, out = 0, []
    for elems, group, row, flip_dim, half in table:
        lo, hi = max(at, start), min(at + elems, start + size)
        if lo < hi:
            cut = half * 128
            a, b = row * 128 + lo - at, row * 128 + hi - at
            if flip_dim:
                a, b = row * 128, row * 128 + elems
            spans = [(a, min(b, cut)), (max(a, cut), b)]
            segs = [(group, int((base >= cut) != (core == 1)), base % cut, end - base) for base, end in spans if base < end]
            out.append((segs, flip_dim, lo - at, hi - at))
        at += elems
    return out


def assemble(table, groups, total):
    n = lax.axis_size(BATCH_AXIS)
    part = total // n

    def branch(d, core):
        def run(*flat_groups):
            res = []
            for segs, flip_dim, lo, hi in chunk_pieces(table, d * part, part, core):
                vals = [flat_groups[2 * g + side].reshape(-1)[o:o + ln] for g, side, o, ln in segs]
                if flip_dim:
                    val = jnp.concatenate(vals).reshape(flip_dim, -1).T.reshape(-1)
                    vals = [val[lo:hi]]
                res += vals
            return jnp.concatenate(res)

        return run

    which = lax.axis_index(BATCH_AXIS) * 2 + lax.axis_index(GROUP_AXIS) % 2
    flat_groups = [a for g in groups for a in g]
    return lax.switch(which, [branch(d, c) for d in range(n) for c in range(2)], *flat_groups)


def tie(*vals):
    return lax.optimization_barrier(vals)


ORDER = ("1i", "1g", "1o", "2i", "2g", "2o", "3q", "3b", "3o", "4q", "4b", "4o", "pu", "pd", "sq", "sb", "sp", "so", "su", "sd")


def block_step(single_blk, pair_blk, mask_blk, d_single_blk, d_pair_blk, *weights):
    (w1i, w1g, w1o, w2i, w2g, w2o, w3q, w3b, w3o, w4q, w4b, w4o, wpu, wpd, wsq, wsb, wsp, wso, wsu, wsd) = weights
    me = lax.axis_index(GROUP_AXIS)
    idx = jnp.bitwise_xor(me, jnp.arange(4, dtype=jnp.int32))
    z0 = pair_blk[0]
    rows = z0.shape[0]
    mask_add = (mask_blk[0].astype(F32) - 1.0) * MASK_PENALTY
    w1t, w2t, w3bt, w4bt, wspt = w1i.T, w2i.T, w3b.T, w4b.T, wsp.T
    both = lax.all_gather(jnp.stack([single_blk[0], d_single_blk[0]]), GROUP_AXIS, axis=1, tiled=True)

    a1, b1 = mul_pre(z0, w1t)
    b1g = gather_rel(b1)
    x1 = mix_all(functools.partial(mix_fwd, idx), a1, b1g)
    z1 = mul_post(x1, z0, w1g, w1o)
    z1c = rows_to_cols(z1)
    a2r, b2r = mul_pre(z1, w2t)
    a2, b2 = mul_pre(z1c, w2t)
    b2g = gather_rel(b2)
    x2 = mix_all(functools.partial(mix_fwd, idx), a2, b2g)
    z2 = mul_post(x2, z1, w2g, w2o)
    bias3 = bias_full(att_bias(z2, w3bt), mask_add)
    d_cols = rows_to_cols(d_pair_blk[0])
    z3 = att_fwd(z2, bias3, w3q, w3o, 4)
    z3, d_cols = tie(z3, d_cols)
    z3 = rows_to_cols(z3)
    bias4 = bias_full(att_bias(z3, w4bt), mask_add)
    z4 = att_fwd(z3, bias4, w4q, w4o, 4).reshape(-1, C)
    z5 = trans_fwd(z4, wpu, wpd, 1024).reshape(rows, T, C)
    biass = bias_full(att_bias(z5, wspt), mask_add[:, None])

    s_all, ds_all, dbias_s, g_sb, g_sq, g_so, g_su, g_sd = single_step(both[0], both[1], biass, wsq, wsb[None], wso, wsu, wsd)
    s_out = lax.dynamic_slice_in_dim(s_all, me * rows, rows)
    ds_in = lax.dynamic_slice_in_dim(ds_all, me * rows, rows)
    dbias_s = jnp.transpose(lax.dynamic_slice_in_dim(dbias_s, me * rows, rows, 1), (1, 0, 2))
    g_sb = jnp.pad(g_sb.reshape(3, 128), ((0, 5), (0, 0)))
    half_s = group_half([g_sq, g_so, g_su, g_sd, g_sb], False)
    half_s, z5 = tie(half_s, z5)
    part_s = scatter_group(half_s)

    dz5, g_sp = att_fin(z5, d_cols, dbias_s, wspt)
    a1g = gather_rel(a1)
    full_s = gather_group(part_s, False)
    dz4, g_pu, g_pd = trans_bwd(z4, dz5.reshape(-1, C), wpu, wpd, 512)
    dz4 = dz4.reshape(rows, T, C)
    pair_out = cols_to_rows(z5)
    dn4, db4, g_4q, g_4o = att_bwd(z3, dz4, bias4, w4q, w4o, 4)
    db4 = scatter_rows(jnp.transpose(db4, (1, 0, 2)))
    dz3, g_4b = att_fin(z3, dz4, db4, w4bt, dn4)
    half_p = group_half([g_pu, g_pd, g_4q, g_4o, g_4b.reshape(-1, 128), g_sp.reshape(-1, 128)], True)
    dz3 = cols_to_rows(dz3)
    half_p, dz3 = tie(half_p, dz3)
    part_p = scatter_group(half_p)
    dn3, db3, g_3q, g_3o = att_bwd(z2, dz3, bias3, w3q, w3o, 4)
    db3, pair_out = tie(db3, pair_out)
    db3 = scatter_rows(jnp.transpose(db3, (1, 0, 2)))
    dz2, g_3b = att_fin(z2, dz3, db3, w3bt, dn3)
    dx2, dgl2, g_2o = mul_post_bwd(x2, z1, dz2, w2g, w2o, 0)
    dx2 = list(dx2)
    full_p = gather_group(part_p, True)
    dx2g = gather_rel(dx2)
    dab2 = mix_all(functools.partial(mix_bwd_in, idx), dx2g, a2r, b2r)
    dz1, g_2i, g_2g = mul_pre_bwd(z1, dz2, [d[0] for d in dab2], [d[1] for d in dab2], dgl2, w2i, w2t, w2g)
    half_i = group_half([g_3q, g_3o, g_3b.reshape(-1, 128), g_2i, g_2g, g_2o], True)
    dx1, dgl1, g_1o, dxp = mul_post_bwd(x1, z0, dz1, w1g, w1o, 1)
    half_i, dxp = tie(half_i, dxp)
    part_i = scatter_group(half_i)
    dxt = flip(lax.all_to_all(dxp, GROUP_AXIS, 1, 0, tiled=True))
    dab1 = mix_all(functools.partial(mix_bwd_out, idx), dx1, dxt, b1g, a1g)
    full_i = gather_group(part_i, True)
    dz0, g_1i, g_1g = mul_pre_bwd(z0, dz1, [d[0] for d in dab1], [d[1] for d in dab1], dgl1, w1i, w1t, w1g)
    half_o = group_half([g_1i, g_1g, g_1o], True)
    full_o = small_group(half_o)

    halves = [full_s[0].shape[0], full_p[0].shape[0], full_i[0].shape[0], full_o[0].shape[0]]
    at = [0, 0, 0, 0]
    place = {}
    for group, names in enumerate((("sq", "so", "su", "sd", "sb"), ("pu", "pd", "4q", "4o", "4b", "sp"), ("3q", "3o", "3b", "2i", "2g", "2o"), ("1i", "1g", "1o"))):
        for name in names:
            w = dict(zip(ORDER, weights))[name]
            place[name] = (w.size, group, at[group], w.shape[-1] if name in ("3b", "4b", "sp") else 0, halves[group])
            at[group] += -(-w.size // 1024) * 8
    table = [place[name] for name in ORDER]
    grad_flat = assemble(table, (full_s, full_p, full_i, full_o), sum(w.size for w in weights))
    return s_out[None], pair_out[None], ds_in[None], dz0[None], grad_flat


def solution(mesh):
    spec_single = P(BATCH_AXIS, GROUP_AXIS, None)
    spec_pair = P(BATCH_AXIS, GROUP_AXIS, None, None)
    spec_mask = P(BATCH_AXIS, None)

    def block_fn(single_rep, pair_rep, token_mask, d_single_out, d_pair_out, *weights):
        in_specs = (spec_single, spec_pair, spec_mask, spec_single, spec_pair) + tuple(P() for w_item in weights)
        out_specs = (spec_single, spec_pair, spec_single, spec_pair, P(BATCH_AXIS))
        mapped = jax.shard_map(block_step, mesh=mesh, in_specs=in_specs, out_specs=out_specs, check_vma=False)
        return mapped(single_rep, pair_rep, token_mask, d_single_out, d_pair_out, *weights)

    return block_fn
```

time: 2150 us -> 1020 us (0.47)
  the two profiles are of different devices: /device:TPU:0 before, /device:TPU:5 now
where the time goes in v1:
time: 1020 us; the launch traced here: 1010 us
  Pallas kernels  407 us (40%)
  waiting for transfers between devices  321 us (31%)
  local copies, waits for them, and re-layouts  117 us (11%)
  starting transfers between devices  84.3 us (8%)
  blocking collectives  46 us (5%)
  other arithmetic  15.2 us (1%)
  between operations  15 us (1%)
    ppermute x21, waiting for transfers between devices, swap_chip(): return lax.ppermute(x_in, GROUP_AXIS, flip_perm(2))  204 us
    pallas_call x2, Pallas kernels, att_bwd(): pl.pallas_call(att_bwd_body, grid=(r // b,), in_specs=[spec, spec, full(b...  84.6 us
    pallas_call x16, Pallas kernels, mix_call(): pl.pallas_call(body, grid_spec=gs, out_shape=[jax.ShapeDtypeStruct((w, r,...  73.1 us
    all_to_all x2, waiting for transfers between devices, cols_to_rows(): lax.all_to_all(jnp.transpose(x_in, (1, 0, 2)), GROUP_AXIS, 0, 1, tiled=True)  48.6 us
    ppermute x41, starting transfers between devices, swap_core(): return lax.ppermute(x_in, GROUP_AXIS, flip_perm(1))  38 us
    pallas_call x2, Pallas kernels, mul_pre_bwd(): pl.pallas_call(mul_pre_bwd_body, grid=(r // RB,), in_specs=cspecs(NCH) *...  37 us
    unnamed x114, local copies, waits for them, and re-layouts  36.9 us
    pallas_call x2, Pallas kernels, mul_post_bwd(): pl.pallas_call(functools.partial(mul_post_bwd_body, pix), grid=(r // RB,)...  36.8 us
  transfers between devices with their start and end apart: 80, of which 32 were waited for; matrix products, arithmetic and copies ran while one was open for 6% of the time, Pallas kernels for 30%

profile of v1, /device:TPU:5, one launch (start us, length us, event | category | flops | bytes accessed | tf_op | source)
XLA Modules:
  0.0 1005.7 jit_solution(18206557308765654858)
XLA Ops:
  22.1 10.0 collective-permute-done.1.b2
  33.6 9.8 collective-permute-done.4.b2
  44.9 9.7 collective-permute-done.7.b2
  56.1 9.8 collective-permute-done.10.b2
  108.3 19.5 %all-to-all-done = bf16[32,128,256]{2,0,1:T(8,128)(2,1)S(1)} async-done(((bf16[32,128,256]{2,0,1:T(8,128)(2,1)}), bf16[32,128,256]{2,0,1:T(8,128)(2,1)S(1)}, u32[]{:S(2)}, u32[]{:S(2)}) %all-to-all-start) | async-done | bytes 2097184 | tf_op jit(solution)/shard_map/all_to_all | solution.py:675
  150.4 19.4 %collective-permute-done.13.b2 = bf16[64,32,128]{2,1,0:T(8,128)(2,1)S(1)} collective-permute-done((bf16[64,32,128]{2,1,0:T(8,128)(2,1)}, bf16[64,32,128]{2,1,0:T(8,128)(2,1)S(1)}, u32[]{:S(2)}, u32[]{:S(2)}) %collective-permute-start.13) | collective-permute-done | bytes 524320 | tf_op jit(solution)/shard_map/ppermute | solution.py:655
  171.4 9.8 collective-permute-done.16.b2
  193.9 9.7 collective-permute-done.22.b2
  245.1 18.3 %att_fwd.2 = bf16[32,128,256]{2,1,0:T(8,128)(2,1)} custom-call(bf16[32,128,256]{2,1,0:T(8,128)(2,1)} %mul_post.3.z_ref, f32[8,128,128]{2,1,0:T(8,128)} %add_bitcast_fusion.2.bias_ref, bf16[256,1024]{1,0:T(8,128)(2,1)} %wq_ref.9, bf16[256,256]{1,0:T(8,128)(2,1)} %wo_ref.9), custom_call_target="tpu_custom_call" | custom-call | flops 4294967296 | bytes 8388608 | tf_op jit(solution)/shard_map/att_fwd/pallas_call | solution.py:219
  272.0 26.8 %all_gather.27 = bf16[2,128,384]{2,1,0:T(8,128)(2,1)S(1)} all-gather(bf16[2,32,384]{2,1,0:T(8,128)(2,1)S(1)} %pad_maximum_fusion.2), channel_id=1, replica_groups=mesh['dp'=8,'dap'=4] {'dap'}, dimensions={1}, use_global_device_ids=true | all-gather | bytes 245760 | tf_op jit(solution)/shard_map/all_gather | solution.py:796
  313.1 18.3 %att_fwd.3 = bf16[32,128,256]{2,1,0:T(8,128)(2,1)} custom-call(bf16[32,128,256]{2,1,0:T(8,128)(2,1)} %bitcast.206, f32[8,128,128]{2,1,0:T(8,128)} %add_bitcast_fusion.1.bias_ref, bf16[256,1024]{1,0:T(8,128)(2,1)} %wq_ref.8, bf16[256,256]{1,0:T(8,128)(2,1)} %wo_ref.8), custom_call_target="tpu_custom_call" | custom-call | flops 4294967296 | bytes 8388608 | tf_op jit(solution)/shard_map/att_fwd/pallas_call | solution.py:219
  331.4 12.9 %trans_fwd.1 = bf16[4096,256]{1,0:T(8,128)(2,1)} custom-call(bf16[4096,256]{1,0:T(8,128)(2,1)} %bitcast.241, bf16[256,2048]{1,0:T(8,128)(2,1)} %wu_ref.5, bf16[1024,256]{1,0:T(8,128)(2,1)} %wd_ref.5), custom_call_target="tpu_custom_call" | custom-call | flops 4294967296 | bytes 8388608 | tf_op jit(solution)/shard_map/trans_fwd/pallas_call | solution.py:123
  358.0 11.9 %single_step.1 = (bf16[128,384]{1,0:T(8,128)(2,1)}, bf16[128,384]{1,0:T(8,128)(2,1)}, f32[16,128,128]{2,1,0:T(8,128)}, f32[1,384]{1,0:T(1,128)}, f32[4608,128]{1...) custom-call(bf16[128,384]{1,0:T(8,128)(2,1)} %get-tuple-element.337.s_ref, ...), custom_call_target="tpu_custom_call" | custom-call | flops 8589934592 | bytes 16777216 | tf_op jit(solution)/shard_map/single_step/pallas_call | solution.py:641
  393.0 30.1 %trans_bwd.1 = (bf16[4096,256]{1,0:T(8,128)(2,1)}, f32[4096,128]{1,0:T(8,128)}, f32[2048,128]{1,0:T(8,128)}) custom-call(bf16[4096,256]{1,0:T(8,128)(2,1)} %bitcast.242, bf16[4096,256]{1,0:T(8,128)(2,1)} %bitcast.245, bf16[256,2048]{1,0:T(8,128)(2,1)} %wu_ref.5, bf16[1024,256]{1,0:T(8,128)(2,1)} %wd_ref.5), custom_call_target="tpu_custom_call" | custom-call | flops 4294967296 | bytes 8388608 | tf_op jit(solution)/shard_map/trans_bwd/pallas_call | solution.py:130
  423.1 42.4 %att_bwd.2 = (f32[4096,256]{1,0:T(8,128)}, f32[8,128,128]{2,1,0:T(8,128)}, f32[2048,128]{1,0:T(8,128)}, f32[512,128]{1,0:T(8,128)}) custom-call(bf16[32,128,256]{2,1,0:T(8,128)(2,1)} %bitcast.207, bf16[32,128,256]{2,1,0:T(8,128)(2,1)} %bitcast.243, f32[8,128,128]{2,1,0:T(8,128)} %add_bitcast_fusion.1.bias_ref, bf16[256,1024]{1,0:T(8,128)(2,1)} %wq_ref.8, ...), custom_call_target="tpu_custom_call" | custom-call | flops 4294967296 | bytes 8388608 | tf_op jit(solution)/shard_map/att_bwd/pallas_call | solution.py:290
  498.2 24.7 %all-to-all-done.3 = bf16[128,32,256]{2,1,0:T(8,128)(2,1)S(1)} async-done(((bf16[128,32,256]{2,1,0:T(8,128)(2,1)}), bf16[128,32,256]{2,1,0:T(8,128)(2,1)S(1)}, u32[]{:S(2)}, u32[]{:S(2)}) %all-to-all-start.3) | async-done | bytes 2097184 | tf_op jit(solution)/shard_map/all_to_all | solution.py:679
  537.8 23.9 %all-to-all-done.4 = bf16[128,32,256]{2,1,0:T(8,128)(2,1)S(1)} async-done(((bf16[128,32,256]{2,1,0:T(8,128)(2,1)}), bf16[128,32,256]{2,1,0:T(8,128)(2,1)S(1)}, u32[]{:S(2)}, u32[]{:S(2)}) %all-to-all-start.4) | async-done | bytes 2097184 | tf_op jit(solution)/shard_map/all_to_all | solution.py:679
  563.3 42.2 %att_bwd.3 = (f32[4096,256]{1,0:T(8,128)}, f32[8,128,128]{2,1,0:T(8,128)}, f32[2048,128]{1,0:T(8,128)}, f32[512,128]{1,0:T(8,128)}) custom-call(bf16[32,128,256]{2,1,0:T(8,128)(2,1)} %mul_post.3.z_ref, bf16[32,128,256]{2,1,0:T(8,128)(2,1)} %bitcast.209, f32[8,128,128]{2,1,0:T(8,128)} %add_bitcast_fusion.2.bias_ref, bf16[256,1024]{1,0:T(8,128)(2,1)} %wq_ref.9, ...), custom_call_target="tpu_custom_call" | custom-call | flops 4294967296 | bytes 8388608 | tf_op jit(solution)/shard_map/att_bwd/pallas_call | solution.py:290
  624.9 18.1 %mul_post_bwd.2 = (bf16[64,32,128]{2,1,0:T(8,128)(2,1)}, bf16[64,32,128]{2,1,0:T(8,128)(2,1)}, bf16[64,32,128]{2,1,0:T(8,128)(2,1)}, bf16[64,32,128]{2,1,0:T(8,1...) custom-call(f32[64,32,128]{2,1,0:T(8,128)} %shard_map.276.refs_0_, f32[64,32,128]{2,1,0:T(8,128)} %shard_map.277.refs_1_, ...), custom_call_target="tpu_custom_call" | custom-call | flops 4294967296 | bytes 8388608 | tf_op jit(solution)/shard_map/mul_post_bwd/pallas_call | solution.py:499
  646.8 10.2 %collective-permute-done.30.d2 = bf16[64,32,128]{2,1,0:T(8,128)(2,1)} collective-permute-done((bf16[64,32,128]{2,1,0:T(8,128)(2,1)}, bf16[64,32,128]{2,1,0:T(8,128)(2,1)}, u32[]{:S(2)}, u32[]{:S(2)}) %collective-permute-start.30) | collective-permute-done | bytes 524320 | tf_op jit(solution)/shard_map/ppermute | solution.py:655
  669.9 9.7 collective-permute-done.36.d2
  712.0 18.4 %mul_pre_bwd.2 = (bf16[32,128,256]{2,1,0:T(8,128)(2,1)}, f32[2048,128]{1,0:T(8,128)}, f32[512,128]{1,0:T(8,128)}) custom-call(bf16[64,32,128]{2,1,0:T(8,128)(2,1)} %get-tuple-element.273.refs_0_, bf16[64,32,128]{2,1,0:T(8,128)(2,1)} %get-tuple-element.277.refs_1_, bf16[64,32,128]{2,1,0:T(8,128)(2,1)} %get-tuple-element.281.refs_2_, ...), custom_call_target="tpu_custom_call" | custom-call | flops 4294967296 | bytes 8388608 | tf_op jit(solution)/shard_map/mul_pre_bwd/pallas_call | solution.py:568
  734.5 18.8 %mul_post_bwd.3 = (bf16[64,32,128]{2,1,0:T(8,128)(2,1)}, bf16[64,32,128]{2,1,0:T(8,128)(2,1)}, bf16[64,32,128]{2,1,0:T(8,128)(2,1)}, bf16[64,32,128]{2,1,0:T(8,1...) custom-call(f32[64,32,128]{2,1,0:T(8,128)} %shard_map.272.refs_0_, ...), custom_call_target="tpu_custom_call" | custom-call | flops 4294967296 | bytes 8388608 | tf_op jit(solution)/shard_map/mul_post_bwd/pallas_call | solution.py:499
  765.2 29.4 %collective-permute-done.65 = f32[552,128]{1,0:T(8,128)S(1)} collective-permute-done((f32[552,128]{1,0:T(8,128)}, f32[552,128]{1,0:T(8,128)S(1)}, u32[]{:S(2)}, u32[]{:S(2)}) %collective-permute-start.65) | collective-permute-done | bytes 282656 | tf_op jit(solution)/shard_map/ppermute | solution.py:655
  801.0 10.1 %collective-permute-done.43.a2 = bf16[64,32,128]{2,1,0:T(8,128)(2,1)} collective-permute-done((bf16[64,32,128]{2,1,0:T(8,128)(2,1)}, bf16[64,32,128]{2,1,0:T(8,128)(2,1)}, u32[]{:S(2)}, u32[]{:S(2)}) %collective-permute-start.43) | collective-permute-done | bytes 524320 | tf_op jit(solution)/shard_map/ppermute | solution.py:655
  812.6 9.8 collective-permute-done.46.a2
  835.0 9.8 collective-permute-done.52.a2
  872.7 18.5 %mul_pre_bwd.3 = (bf16[32,128,256]{2,1,0:T(8,128)(2,1)}, f32[2048,128]{1,0:T(8,128)}, f32[512,128]{1,0:T(8,128)}) custom-call(bf16[64,32,128]{2,1,0:T(8,128)(2,1)} %get-tuple-element.302.refs_0_, bf16[64,32,128]{2,1,0:T(8,128)(2,1)} %get-tuple-element.305.refs_1_, bf16[64,32,128]{2,1,0:T(8,128)(2,1)} %get-tuple-element.308.refs_2_, ...), custom_call_target="tpu_custom_call" | custom-call | flops 4294967296 | bytes 8388608 | tf_op jit(solution)/shard_map/mul_pre_bwd/pallas_call | solution.py:568
  932.3 11.6 %collective-permute-done.59 = f32[192,128]{1,0:T(8,128)S(1)} collective-permute-done((f32[192,128]{1,0:T(8,128)S(1)}, f32[192,128]{1,0:T(8,128)S(1)}, u32[]{:S(2)}, u32[]{:S(2)}) %collective-permute-start.59) | collective-permute-done | bytes 98336 | tf_op jit(solution)/shard_map/ppermute | solution.py:736
  954.2 9.8 collective-permute-done.61
  967.7 31.1 %conditional.1 = (f32[592944]{0:T(1024)}) conditional(s32[]{:T(128)} %clamp.3, (f32[1536,128]{1,0:T(8,128)S(1)}, f32[1536,128]{1,0:T(8,128)}, f32[2880,128]{1,0:T(8,128)}, f32[2880,128]{1,0:T(8,128)}) %tuple.66, (f32[1536,128]{1,0:T(8,128)}, f32[1536,128]{1,0:T(8,128)S(1)}, f32[2880,128]{1,0:T(8,128)}, ...), branch_computations={%region_3.4_spmd, %region_4.5_spmd, %region_5.6_spmd, %region_6.7_... | conditional | flops 592944 | bytes 15434532 | solution.py:778
  974.5 24.2 %concatenate.39 = f32[592944]{0:T(1024)} concatenate(f32[62416]{0:T(1024)} %slice.282, f32[65536]{0:T(1024)} %get-tuple-element.330, f32[65536]{0:T(1024)} %get-tuple-element.329, f32[262144]{0:T(1024)S(1)} %slice_bitcast_fusion.4, f32[2048]{0:T(1024)S(1)} %reshape.211, f32[65536]{0:T(1024)} %get-tuple-element.331, f32[69728]{0:T(1024)} %slice.283), dimensions={0} | concatenate | bytes 4743552 | tf_op jit(solution)/shard_map/cond/branch_3_fun/concatenate | solution.py:772
  (368 shorter events, 443.1 us)
Async XLA Ops:
  20.6 34.0 %collective-permute-start.7 = (bf16[64,32,128]{2,1,0:T(8,128)(2,1)}, bf16[64,32,128]{2,1,0:T(8,128)(2,1)S(1)}, u32[]{:S(2)}, u32[]{:S(2)}) collective-permute-start(bf16[64,32,128]{2,1,0:T(8,128)(2,1)} %get-tuple-element.231.b0), channel_id=1, source_target_pairs={{0,2},{1,3},{2,0},{3,1},{4,6},{5,7},{6,4},{7,5},{8,10},{9,11},{10,... | collective-permute-start | bytes 1572872 | tf_op jit(solution)/shard_map/ppermute | solution.py:655
  21.8 44.0 %collective-permute-start.10 = (bf16[64,32,128]{2,1,0:T(8,128)(2,1)}, bf16[64,32,128]{2,1,0:T(8,128)(2,1)S(1)}, u32[]{:S(2)}, u32[]{:S(2)}) collective-permute-start(bf16[64,32,128]{2,1,0:T(8,128)(2,1)} %get-tuple-element.233.b0), channel_id=1, source_target_pairs={{0,2},{1,3},{2,0},{3,1},{4,6},{5,7},{6,4},{7,5},{8,10},{9,11},{10,... | collective-permute-start | bytes 1572872 | tf_op jit(solution)/shard_map/ppermute | solution.py:655
  32.1 34.6 %collective-permute-start.2 = (bf16[64,32,128]{2,1,0:T(8,128)(2,1)S(1)}, bf16[64,32,128]{2,1,0:T(8,128)(2,1)S(1)}, u32[]{:S(2)}, u32[]{:S(2)}) collective-permute-start(bf16[64,32,128]{2,1,0:T(8,128)(2,1)S(1)} %collective-permute-done.1.b2), channel_id=1, source_target_pairs={{0,1},{1,0},{2,3},{3,2},{4,5},{5,4},{6,7},{7,6},{8,9},{9,8},{10,11... | collective-permute-start | bytes 1572872 | tf_op jit(solution)/shard_map/ppermute | solution.py:651
  44.8 31.9 %collective-permute-start.6 = (bf16[64,32,128]{2,1,0:T(8,128)(2,1)}, bf16[64,32,128]{2,1,0:T(8,128)(2,1)}, u32[]{:S(2)}, u32[]{:S(2)}) collective-permute-start(bf16[64,32,128]{2,1,0:T(8,128)(2,1)} %get-tuple-element.231.b0), channel_id=1, source_target_pairs={{0,1},{1,0},{2,3},{3,2},{4,5},{5,4},{6,7},{7,6},{8,9},{9,8},{10,11... | collective-permute-start | bytes 1572872 | tf_op jit(solution)/shard_map/ppermute | solution.py:651
  129.2 76.2 %all-to-all-start.1 = ((bf16[32,128,256]{2,0,1:T(8,128)(2,1)}), bf16[32,128,256]{2,0,1:T(8,128)(2,1)S(1)}, u32[]{:S(2)}, u32[]{:S(2)}) async-start(bf16[32,128,256]{2,0,1:T(8,128)(2,1)} %bitcast.178), calls=%async_computation.1 | async-start | bytes 4194304 | tf_op jit(solution)/shard_map/all_to_all | solution.py:675
  147.4 33.8 %collective-permute-start.16 = (bf16[64,32,128]{2,1,0:T(8,128)(2,1)}, bf16[64,32,128]{2,1,0:T(8,128)(2,1)}, u32[]{:S(2)}, u32[]{:S(2)}) collective-permute-start(bf16[64,32,128]{2,1,0:T(8,128)(2,1)} %get-tuple-element.237.b0), channel_id=1, source_target_pairs={{0,2},{1,3},{2,0},{3,1},{4,6},{5,7},{6,4},{7,5},{8,10},{9,11},{10,... | collective-permute-start | bytes 1572872 | tf_op jit(solution)/shard_map/ppermute | solution.py:655
  147.4 35.4 %collective-permute-start.15 = (bf16[64,32,128]{2,1,0:T(8,128)(2,1)}, bf16[64,32,128]{2,1,0:T(8,128)(2,1)S(1)}, u32[]{:S(2)}, u32[]{:S(2)}) collective-permute-start(bf16[64,32,128]{2,1,0:T(8,128)(2,1)} %get-tuple-element.237.b0), channel_id=1, source_target_pairs={{0,1},{1,0},{2,3},{3,2},{4,5},{5,4},{6,7},{7,6},{8,9},{9,8},{10,11... | collective-permute-start | bytes 1572872 | tf_op jit(solution)/shard_map/ppermute | solution.py:651
  148.2 44.2 %collective-permute-start.19 = (bf16[64,32,128]{2,1,0:T(8,128)(2,1)}, bf16[64,32,128]{2,1,0:T(8,128)(2,1)S(1)}, u32[]{:S(2)}, u32[]{:S(2)}) collective-permute-start(bf16[64,32,128]{2,1,0:T(8,128)(2,1)} %get-tuple-element.239.b0), channel_id=1, source_target_pairs={{0,2},{1,3},{2,0},{3,1},{4,6},{5,7},{6,4},{7,5},{8,10},{9,11},{10,... | collective-permute-start | bytes 1572872 | tf_op jit(solution)/shard_map/ppermute | solution.py:655
  150.3 53.3 %collective-permute-start.22 = (bf16[64,32,128]{2,1,0:T(8,128)(2,1)}, bf16[64,32,128]{2,1,0:T(8,128)(2,1)S(1)}, u32[]{:S(2)}, u32[]{:S(2)}) collective-permute-start(bf16[64,32,128]{2,1,0:T(8,128)(2,1)} %get-tuple-element.241.b0), channel_id=1, source_target_pairs={{0,2},{1,3},{2,0},{3,1},{4,6},{5,7},{6,4},{7,5},{8,10},{9,11},{10,... | collective-permute-start | bytes 1572872 | tf_op jit(solution)/shard_map/ppermute | solution.py:655
  169.9 34.7 %collective-permute-start.14 = (bf16[64,32,128]{2,1,0:T(8,128)(2,1)S(1)}, bf16[64,32,128]{2,1,0:T(8,128)(2,1)S(1)}, u32[]{:S(2)}, u32[]{:S(2)}) collective-permute-start(bf16[64,32,128]{2,1,0:T(8,128)(2,1)S(1)} %collective-permute-done.13.b2), channel_id=1, source_target_pairs={{0,1},{1,0},{2,3},{3,2},{4,5},{5,4},{6,7},{7,6},{8,9},{9,8},{10,11... | collective-permute-start | bytes 1572872 | tf_op jit(solution)/shard_map/ppermute | solution.py:651
  182.7 32.8 %collective-permute-start.18 = (bf16[64,32,128]{2,1,0:T(8,128)(2,1)}, bf16[64,32,128]{2,1,0:T(8,128)(2,1)}, u32[]{:S(2)}, u32[]{:S(2)}) collective-permute-start(bf16[64,32,128]{2,1,0:T(8,128)(2,1)} %get-tuple-element.239.b0), channel_id=1, source_target_pairs={{0,1},{1,0},{2,3},{3,2},{4,5},{5,4},{6,7},{7,6},{8,9},{9,8},{10,11... | collective-permute-start | bytes 1572872 | tf_op jit(solution)/shard_map/ppermute | solution.py:651
  267.6 32.0 %all-to-all-start.2 = ((bf16[32,128,256]{2,0,1:T(8,128)(2,1)}), bf16[32,128,256]{2,0,1:T(8,128)(2,1)S(1)}, u32[]{:S(2)}, u32[]{:S(2)}) async-start(bf16[32,128,256]{2,0,1:T(8,128)(2,1)} %copy.81), calls=%async_computation.2 | async-start | bytes 4194304 | tf_op jit(solution)/shard_map/all_to_all | solution.py:675
  271.4 265.6 %reduce-scatter.8.cloned.1.call-start = ((), (), s32[]{:S(2)}) async-start(), calls=%async_computation.11 | async-start | bytes 5677056 | tf_op jit(solution)/shard_map/reduce_scatter | solution.py:709
  491.6 32.9 %collective-permute-start.26 = (f32[4416,128]{1,0:T(8,128)}, f32[4416,128]{1,0:T(8,128)}, u32[]{:S(2)}, u32[]{:S(2)}) collective-permute-start(f32[4416,128]{1,0:T(8,128)} %constant_dynamic-slice_fusion.7), channel_id=1, source_target_pairs={{0,1},{1,0},{2,3},{3,2},{4,5},{5,4},{6,7},{7,6},{8,9},{9,8},{10,11... | collective-permute-start | bytes 6782984 | tf_op jit(solution)/shard_map/ppermute | solution.py:651
  498.2 265.7 %reduce-scatter.12.cloned.1.call-start = ((), (), s32[]{:S(2)}) async-start(), calls=%async_computation.14 | async-start | bytes 2543616
  537.1 357.1 %all-gather.8.cloned.1.call-start = ((), (), s32[]{:S(2)}) async-start(), calls=%async_computation.12 | async-start | bytes 5677056 | tf_op jit(solution)/shard_map/all_gather | solution.py:715
  537.8 356.5 %reduce-scatter.10.cloned.1.call-start = ((), (), s32[]{:S(2)}) async-start(), calls=%async_computation.13 | async-start | bytes 1658880
  645.3 34.3 %collective-permute-start.36 = (bf16[64,32,128]{2,1,0:T(8,128)(2,1)}, bf16[64,32,128]{2,1,0:T(8,128)(2,1)}, u32[]{:S(2)}, u32[]{:S(2)}) collective-permute-start(bf16[64,32,128]{2,1,0:T(8,128)(2,1)} %get-tuple-element.280.d0), channel_id=1, source_target_pairs={{0,2},{1,3},{2,0},{3,1},{4,6},{5,7},{6,4},{7,5},{8,10},{9,11},{10,... | collective-permute-start | bytes 1572872 | tf_op jit(solution)/shard_map/ppermute | solution.py:655
  645.8 45.0 %collective-permute-start.39 = (bf16[64,32,128]{2,1,0:T(8,128)(2,1)}, bf16[64,32,128]{2,1,0:T(8,128)(2,1)}, u32[]{:S(2)}, u32[]{:S(2)}) collective-permute-start(bf16[64,32,128]{2,1,0:T(8,128)(2,1)} %get-tuple-element.284.d0), channel_id=1, source_target_pairs={{0,2},{1,3},{2,0},{3,1},{4,6},{5,7},{6,4},{7,5},{8,10},{9,11},{10,... | collective-permute-start | bytes 1572872 | tf_op jit(solution)/shard_map/ppermute | solution.py:655
  657.1 34.7 %collective-permute-start.31 = (bf16[64,32,128]{2,1,0:T(8,128)(2,1)}, bf16[64,32,128]{2,1,0:T(8,128)(2,1)}, u32[]{:S(2)}, u32[]{:S(2)}) collective-permute-start(bf16[64,32,128]{2,1,0:T(8,128)(2,1)} %collective-permute-done.30.d2), channel_id=1, source_target_pairs={{0,1},{1,0},{2,3},{3,2},{4,5},{5,4},{6,7},{7,6},{8,9},{9,8},{10,11... | collective-permute-start | bytes 1572872 | tf_op jit(solution)/shard_map/ppermute | solution.py:651
  667.3 34.5 %collective-permute-start.35 = (bf16[64,32,128]{2,1,0:T(8,128)(2,1)}, bf16[64,32,128]{2,1,0:T(8,128)(2,1)}, u32[]{:S(2)}, u32[]{:S(2)}) collective-permute-start(bf16[64,32,128]{2,1,0:T(8,128)(2,1)} %get-tuple-element.280.d0), channel_id=1, source_target_pairs={{0,1},{1,0},{2,3},{3,2},{4,5},{5,4},{6,7},{7,6},{8,9},{9,8},{10,11... | collective-permute-start | bytes 1572872 | tf_op jit(solution)/shard_map/ppermute | solution.py:651
  760.0 63.8 %all-to-all-start.5 = ((bf16[32,128,256]{2,0,1:T(8,128)(2,1)}), bf16[32,128,256]{2,0,1:T(8,128)(2,1)S(1)}, u32[]{:S(2)}, u32[]{:S(2)}) async-start(bf16[32,128,256]{2,0,1:T(8,128)(2,1)} %copy.94), calls=%async_computation.5 | async-start | bytes 4194304 | tf_op jit(solution)/shard_map/all_to_all | solution.py:854
  763.8 160.2 %all-gather.6.cloned.1.call-start = ((), (), s32[]{:S(2)}) async-start(), calls=%async_computation.10 | async-start | bytes 2543616 | tf_op jit(solution)/shard_map/all_gather | solution.py:715
  796.3 154.8 %all-gather.4.cloned.1.call-start = ((), (), s32[]{:S(2)}) async-start(), calls=%async_computation.9 | async-start | bytes 1658880 | tf_op jit(solution)/shard_map/all_gather | solution.py:715
  799.5 34.1 %collective-permute-start.49 = (bf16[64,32,128]{2,1,0:T(8,128)(2,1)S(1)}, bf16[64,32,128]{2,1,0:T(8,128)(2,1)}, u32[]{:S(2)}, u32[]{:S(2)}) collective-permute-start(bf16[64,32,128]{2,1,0:T(8,128)(2,1)S(1)} %copy-done.14), channel_id=1, source_target_pairs={{0,2},{1,3},{2,0},{3,1},{4,6},{5,7},{6,4},{7,5},{8,10},{9,11},{10,... | collective-permute-start | bytes 1572872 | tf_op jit(solution)/shard_map/ppermute | solution.py:655
  799.6 45.2 %collective-permute-start.52 = (bf16[64,32,128]{2,1,0:T(8,128)(2,1)S(1)}, bf16[64,32,128]{2,1,0:T(8,128)(2,1)}, u32[]{:S(2)}, u32[]{:S(2)}) collective-permute-start(bf16[64,32,128]{2,1,0:T(8,128)(2,1)S(1)} %copy-done.13), channel_id=1, source_target_pairs={{0,2},{1,3},{2,0},{3,1},{4,6},{5,7},{6,4},{7,5},{8,10},{9,11},{10,... | collective-permute-start | bytes 1572872 | tf_op jit(solution)/shard_map/ppermute | solution.py:655
  811.1 34.6 %collective-permute-start.44 = (bf16[64,32,128]{2,1,0:T(8,128)(2,1)}, bf16[64,32,128]{2,1,0:T(8,128)(2,1)}, u32[]{:S(2)}, u32[]{:S(2)}) collective-permute-start(bf16[64,32,128]{2,1,0:T(8,128)(2,1)} %collective-permute-done.43.a2), channel_id=1, source_target_pairs={{0,1},{1,0},{2,3},{3,2},{4,5},{5,4},{6,7},{7,6},{8,9},{9,8},{10,11... | collective-permute-start | bytes 1572872 | tf_op jit(solution)/shard_map/ppermute | solution.py:651
  822.3 33.9 %collective-permute-start.47 = (bf16[64,32,128]{2,1,0:T(8,128)(2,1)}, bf16[64,32,128]{2,1,0:T(8,128)(2,1)}, u32[]{:S(2)}, u32[]{:S(2)}) collective-permute-start(bf16[64,32,128]{2,1,0:T(8,128)(2,1)} %collective-permute-done.46.a2), channel_id=1, source_target_pairs={{0,1},{1,0},{2,3},{3,2},{4,5},{5,4},{6,7},{7,6},{8,9},{9,8},{10,11... | collective-permute-start | bytes 1572872 | tf_op jit(solution)/shard_map/ppermute | solution.py:651
  826.3 34.8 %collective-permute-start.48 = (bf16[64,32,128]{2,1,0:T(8,128)(2,1)S(1)}, bf16[64,32,128]{2,1,0:T(8,128)(2,1)S(1)}, u32[]{:S(2)}, u32[]{:S(2)}) collective-permute-start(bf16[64,32,128]{2,1,0:T(8,128)(2,1)S(1)} %copy-done.14), channel_id=1, source_target_pairs={{0,1},{1,0},{2,3},{3,2},{4,5},{5,4},{6,7},{7,6},{8,9},{9,8},{10,11... | collective-permute-start | bytes 1572872 | tf_op jit(solution)/shard_map/ppermute | solution.py:651
  833.6 33.3 %collective-permute-start.51 = (bf16[64,32,128]{2,1,0:T(8,128)(2,1)S(1)}, bf16[64,32,128]{2,1,0:T(8,128)(2,1)S(1)}, u32[]{:S(2)}, u32[]{:S(2)}) collective-permute-start(bf16[64,32,128]{2,1,0:T(8,128)(2,1)S(1)} %copy-done.13), channel_id=1, source_target_pairs={{0,1},{1,0},{2,3},{3,2},{4,5},{5,4},{6,7},{7,6},{8,9},{9,8},{10,11... | collective-permute-start | bytes 1572872 | tf_op jit(solution)/shard_map/ppermute | solution.py:651
  894.2 73.5 %collective-permute-start.67 = (f32[9856,128]{1,0:T(8,128)}, f32[9856,128]{1,0:T(8,128)}, u32[]{:S(2)}, u32[]{:S(2)}) collective-permute-start(f32[9856,128]{1,0:T(8,128)} %all-gather.8.cloned.1.call-done), channel_id=1, source_target_pairs={{0,1},{1,0},{2,3},{3,2},{4,5},{5,4},{6,7},{7,6},{8,9},{9,8},{10,11... | collective-permute-start | bytes 15138824 | tf_op jit(solution)/shard_map/ppermute | solution.py:651
  924.0 43.6 %collective-permute-start.66 = (f32[4416,128]{1,0:T(8,128)}, f32[4416,128]{1,0:T(8,128)}, u32[]{:S(2)}, u32[]{:S(2)}) collective-permute-start(f32[4416,128]{1,0:T(8,128)} %all-gather.6.cloned.1.call-done), channel_id=1, source_target_pairs={{0,1},{1,0},{2,3},{3,2},{4,5},{5,4},{6,7},{7,6},{8,9},{9,8},{10,11... | collective-permute-start | bytes 6782984 | tf_op jit(solution)/shard_map/ppermute | solution.py:651
  (94 other events, 1480.1 us)
Sparse Core Ops, SparseCore 0:
  383.9 100.1 reduce-scatter.7
  528.6 67.3 reduce-scatter.11
  598.2 82.2 all-gather.7
  756.1 61.6 reduce-scatter.9
  819.8 49.3 all-gather.5
  902.1 49.0 all-gather.3

commit v2 on v1

--- a/solution.py
+++ b/solution.py
@@ -30,24 +30,33 @@
     return lax.dot_general(a, b, (((0,), (0,)), ((), ())), preferred_element_type=F32)
 
 
+def row_sum(x):
+    return jnp.sum(x, axis=-1, keepdims=True)
+
+
+def col_sum(x):
+    return jnp.sum(x, axis=0, keepdims=True)
+
+
 def ln_stats(x):
     inv = 1.0 / x.shape[-1]
-    c = x - jnp.sum(x, axis=-1, keepdims=True) * inv
-    r = lax.rsqrt(jnp.sum(c * c, axis=-1, keepdims=True) * inv + NORM_EPS)
+    c = x - row_sum(x) * inv
+    r = lax.rsqrt(row_sum(c * c) * inv + NORM_EPS)
     return c * r, r
 
 
 def ln_back(dn, xh, r):
     inv = 1.0 / dn.shape[-1]
-    m1 = jnp.sum(dn, axis=-1, keepdims=True) * inv
-    m2 = jnp.sum(dn * xh, axis=-1, keepdims=True) * inv
+    m1 = row_sum(dn) * inv
+    m2 = row_sum(dn * xh) * inv
     return r * (dn - m1 - xh * m2)
 
 
-def put_flat(ref, val):
+def put_flat(ref, val, row=0):
     n = val.shape[1] // 128
     for t in range(n):
-        ref[pl.ds(t, val.shape[0], stride=n), :] = val[:, t * 128:(t + 1) * 128]
+        ref[pl.ds(row + t, val.shape[0], stride=n), :] = val[:, t * 128:(t + 1) * 128]
+    return row + val.size // 128
 
 
 def flat_shape(w):
@@ -62,14 +71,25 @@
     return 1.0 / (1.0 + jnp.exp(-x))
 
 
-def trans_fwd_body(z_ref, wu_ref, wd_ref, o_ref):
+def bias_spec(wbt):
+    return pl.BlockSpec((8, wbt.shape[0], T), lambda i: (i, 0, 0))
+
+
+def bias_shape(r, wbt):
+    return jax.ShapeDtypeStruct((r, wbt.shape[0], T), BF16)
+
+
+def trans_fwd_body(z_ref, wu_ref, wd_ref, wbt_ref, o_ref, b_ref):
     x = z_ref[...].astype(F32)
     xh, _ = ln_stats(x)
     h = mm(xh.astype(BF16), wu_ref[...])
     d = h.shape[1] // 2
     h1 = h[:, :d]
     act = (h1 * sig(h1) * h[:, d:]).astype(BF16)
-    o_ref[...] = (x + mm(act, wd_ref[...])).astype(BF16)
+    o = (x + mm(act, wd_ref[...])).astype(BF16)
+    o_ref[...] = o
+    for i in range(b_ref.shape[0]):
+        b_ref[i] = bias_rows(o[i * T:(i + 1) * T], wbt_ref[...])
 
 
 def trans_bwd_body(z_ref, g_ref, wu_ref, wd_ref, dz_ref, fu_ref, fd_ref, dwu_ref, dwd_ref):
@@ -117,11 +137,12 @@
                 compiler_params=pltpu.CompilerParams(vmem_limit_bytes=60 << 20, dimension_semantics=("arbitrary",)))
 
 
-def trans_fwd(z, wu, wd, blk):
+def trans_fwd(z, wu, wd, wbt):
     p, c = z.shape
+    blk = 8 * T
     spec = pl.BlockSpec((blk, c), lambda i: (i, 0))
-    return pl.pallas_call(trans_fwd_body, grid=(p // blk,), in_specs=[spec, full(wu), full(wd)], out_specs=spec,
-                          out_shape=jax.ShapeDtypeStruct((p, c), BF16), name="trans_fwd", **cp(p * c * WORK))(z, wu, wd)
+    return pl.pallas_call(trans_fwd_body, grid=(p // blk,), in_specs=[spec, full(wu), full(wd), full(wbt)], out_specs=[spec, bias_spec(wbt)],
+                          out_shape=[jax.ShapeDtypeStruct((p, c), BF16), bias_shape(p // T, wbt)], name="trans_fwd", **cp(p * c * WORK))(z, wu, wd, wbt)
 
 
 def trans_bwd(z, g, wu, wd, blk):
@@ -170,7 +191,7 @@
 
 def softmax(s):
     e = jnp.exp(s - jnp.max(s, axis=-1, keepdims=True))
-    return e * (1.0 / jnp.sum(e, axis=-1, keepdims=True))
+    return e * (1.0 / row_sum(e))
 
 
 def stack_heads(x, masks):
@@ -258,7 +279,7 @@
                 blk = (slice(m * T, (m + 1) * T), slice(e * T, (e + 1) * T))
                 p = softmax(lg[blk] + bias_ref[h])
                 pd = p * dp[blk].astype(BF16).astype(F32)
-                dsh = pd - p * jnp.sum(pd, axis=-1, keepdims=True)
+                dsh = pd - p * row_sum(pd)
                 dbias_ref[h] += dsh
                 pp.append(p.astype(BF16))
                 dd.append((dsh * (D ** -0.5)).astype(BF16))
@@ -401,16 +422,14 @@
     return mix_call(mix_fwd_body, idx, [a, *b4], 1, F32, 1)[0]
 
 
-def mix_bwd_out_body(idx_ref, dx_ref, dt_ref, b0, b1, b2, b3, a0, a1, a2, a3, da_ref, db_ref, bb, ab):
-    collect(idx_ref, (b0, b1, b2, b3), bb)
-    collect(idx_ref, (a0, a1, a2, a3), ab)
+def mix_nn_body(idx_ref, x_ref, b0, b1, b2, b3, o_ref, buf):
+    collect(idx_ref, (b0, b1, b2, b3), buf)
     for c in range(CB):
-        da_ref[c] = mm(dx_ref[c], bb[c]).astype(BF16)
-        db_ref[c] = mm(dt_ref[c], ab[c]).astype(BF16)
-
-
-def mix_bwd_out(idx, dx, dxt, b4, a4):
-    return mix_call(mix_bwd_out_body, idx, [dx, dxt, *b4, *a4], 2, BF16, 2)
+        o_ref[c] = mm(x_ref[c], buf[c]).astype(BF16)
+
+
+def mix_nn(idx, x, b4):
+    return mix_call(mix_nn_body, idx, [x, *b4], 1, BF16, 1)[0]
 
 
 def mix_bwd_in_body(idx_ref, a_ref, b_ref, d0, d1, d2, d3, da_ref, db_ref, buf):
@@ -427,15 +446,15 @@
 
 def ln0_stats(x):
     inv = 1.0 / x.shape[0]
-    c = x - jnp.sum(x, axis=0, keepdims=True) * inv
-    r = lax.rsqrt(jnp.sum(c * c, axis=0, keepdims=True) * inv + NORM_EPS)
+    c = x - col_sum(x) * inv
+    r = lax.rsqrt(col_sum(c * c) * inv + NORM_EPS)
     return c * r, r
 
 
 def ln0_back(dn, xh, r):
     inv = 1.0 / dn.shape[0]
-    m1 = jnp.sum(dn, axis=0, keepdims=True) * inv
-    m2 = jnp.sum(dn * xh, axis=0, keepdims=True) * inv
+    m1 = col_sum(dn) * inv
+    m2 = col_sum(dn * xh) * inv
     return r * (dn - m1 - xh * m2)
 
 
@@ -443,23 +462,32 @@
     return jnp.concatenate([ref[:, i, :] for ref in refs])
 
 
+def bias_rows(x, wbt):
+    xh, _ = ln_stats(x.astype(F32))
+    return mm_nt(wbt, xh.astype(BF16)).astype(BF16)
+
+
 def mul_post_body(*refs):
-    xs, (z_ref, wg_ref, wo_ref, o_ref) = refs[:NCH], refs[NCH:]
+    xs, (z_ref, wg_ref, wo_ref), rest = refs[:NCH], refs[NCH:NCH + 3], refs[NCH + 3:]
+    wbt_ref, o_ref, b_ref = rest if len(rest) == 3 else (None, *rest, None)
     for i in range(z_ref.shape[0]):
         z = z_ref[i].astype(F32)
         n, _ = ln_stats(z)
         g = sig(mm(n.astype(BF16), wg_ref[...]))
         xn, _ = ln0_stats(col_of(xs, i))
-        o_ref[i] = (z + g * mm_tn(xn.astype(BF16), wo_ref[...])).astype(BF16)
-
-
-def mul_post(xs, z3, wg, wo):
+        o = (z + g * mm_tn(xn.astype(BF16), wo_ref[...])).astype(BF16)
+        o_ref[i] = o
+        if wbt_ref is not None:
+            b_ref[i] = bias_rows(o, wbt_ref[...])
+
+
+def mul_post(xs, z3, wg, wo, *wbt):
     r = z3.shape[0]
     b = 8
     zs = row_spec(b)
     xspec = pl.BlockSpec((C // NCH, b, T), lambda i: (0, i, 0))
-    return pl.pallas_call(mul_post_body, grid=(r // b,), in_specs=[xspec] * NCH + [zs, full(wg), full(wo)],
-                          out_specs=zs, out_shape=jax.ShapeDtypeStruct((r, T, C), BF16), name="mul_post", **cp(r * T * C * WORK))(*xs, z3, wg, wo)
+    return pl.pallas_call(mul_post_body, grid=(r // b,), in_specs=[xspec] * NCH + [zs, full(wg), full(wo)] + [full(w) for w in wbt],
+                          out_specs=[zs] + [bias_spec(w) for w in wbt], out_shape=[jax.ShapeDtypeStruct((r, T, C), BF16)] + [bias_shape(r, w) for w in wbt], name="mul_post", **cp(r * T * C * WORK))(*xs, z3, wg, wo, *wbt)
 
 
 def mul_post_bwd_body(pix, *refs):
@@ -577,7 +605,7 @@
 
 
 def single_body(s_ref, d_ref, bias_ref, wq_ref, qb_ref, wo_ref, wu_ref, wd_ref,
-                so_ref, ds_ref, dbias_ref, dqb_ref, dwq_ref, dwo_ref, dwu_ref, dwd_ref):
+                so_ref, ds_ref, dbias_ref, flat_ref):
     w = s_ref.shape[1]
     masks = head_masks(w, SD)
     x = s_ref[...].astype(F32)
@@ -610,12 +638,12 @@
     so_ref[...] = (x1 + mm(act, wd_ref[...])).astype(BF16)
     g = d_ref[...]
     da = mm_nt(g, wd_ref[...]).astype(BF16).astype(F32)
-    put_flat(dwd_ref, mm_tn(act, g))
+    g_wd = mm_tn(act, g)
     dh = jnp.concatenate([(da * h2 * (sg + sl * (1.0 - sg))).astype(BF16), (da * sl).astype(BF16)], axis=1)
-    put_flat(dwu_ref, mm_tn(n1, dh))
+    g_wu = mm_tn(n1, dh)
     g1 = (g.astype(F32) + ln_back(mm_nt(dh, wu_ref[...]), xh1, r1)).astype(BF16)
     dgd = mm_nt(g1, wo_ref[...]).astype(BF16).astype(F32)
-    put_flat(dwo_ref, mm_tn(gated, g1))
+    g_wo = mm_tn(gated, g1)
     do = (dgd * gt).astype(BF16)
     dgl = (dgd * o * gt * (1.0 - gt)).astype(BF16)
     dos = stack_heads(do, masks)
@@ -623,22 +651,26 @@
     ds = []
     for h in range(SH):
         pd = pf[h] * dp[h * T:(h + 1) * T].astype(BF16).astype(F32)
-        dsh = pd - pf[h] * jnp.sum(pd, axis=-1, keepdims=True)
+        dsh = pd - pf[h] * row_sum(pd)
         dbias_ref[h] = dsh.T
         ds.append((dsh * (SD ** -0.5)).astype(BF16))
     dq = mm(jnp.concatenate(ds, axis=1), stack_heads(k, masks)).astype(BF16)
     dk = mm_tn(jnp.concatenate(ds), qs).astype(BF16)
     dv = mm_tn(jnp.concatenate(ps), dos).astype(BF16)
-    dqb_ref[...] = jnp.sum(dq.astype(F32), axis=0, keepdims=True)
     dpr = jnp.concatenate([dq, dk, dv, dgl], axis=1)
-    put_flat(dwq_ref, mm_tn(n, dpr))
+    row = 0
+    for val in (mm_tn(n, dpr), g_wo, g_wu, g_wd):
+        row = put_flat(flat_ref, val, row)
+    flat_ref[pl.ds(row, flat_ref.shape[0] - row), :] = jnp.zeros((flat_ref.shape[0] - row, 128), F32)
+    put_flat(flat_ref, col_sum(dq.astype(F32)), row)
     ds_ref[...] = (g1.astype(F32) + ln_back(mm_nt(dpr, wq_ref[...]), xh, r)).astype(BF16)
 
 
 def single_step(s, d, bias, wq, qb, wo, wu, wd):
     vm = pl.BlockSpec(memory_space=pltpu.VMEM)
-    sh = [jax.ShapeDtypeStruct(s.shape, BF16)] * 2 + [jax.ShapeDtypeStruct(a.shape, F32) for a in (bias, qb)] + [flat_shape(a) for a in (wq, wo, wu, wd)]
-    return pl.pallas_call(single_body, in_specs=[vm] * 8, out_specs=[vm] * 8, out_shape=sh, name="single_step",
+    rows = sum(-(-a.size // (128 * 128)) for a in (wq, qb, wo, wu, wd)) * 128
+    sh = [jax.ShapeDtypeStruct(s.shape, BF16)] * 2 + [jax.ShapeDtypeStruct(bias.shape, F32), jax.ShapeDtypeStruct((rows, 128), F32)]
+    return pl.pallas_call(single_body, in_specs=[vm] * 8, out_specs=[vm] * 4, out_shape=sh, name="single_step",
                           cost_estimate=pl.CostEstimate(flops=1 << 33, bytes_accessed=1 << 24, transcendentals=0),
                           compiler_params=pltpu.CompilerParams(vmem_limit_bytes=60 << 20))(s, d, bias, wq, qb, wo, wu, wd)
 
@@ -798,29 +830,29 @@
     a1, b1 = mul_pre(z0, w1t)
     b1g = gather_rel(b1)
     x1 = mix_all(functools.partial(mix_fwd, idx), a1, b1g)
-    z1 = mul_post(x1, z0, w1g, w1o)
+    z1 = mul_post(x1, z0, w1g, w1o)[0]
     z1c = rows_to_cols(z1)
     a2r, b2r = mul_pre(z1, w2t)
     a2, b2 = mul_pre(z1c, w2t)
     b2g = gather_rel(b2)
     x2 = mix_all(functools.partial(mix_fwd, idx), a2, b2g)
-    z2 = mul_post(x2, z1, w2g, w2o)
-    bias3 = bias_full(att_bias(z2, w3bt), mask_add)
+    z2, bias_z2 = mul_post(x2, z1, w2g, w2o, w3bt)
+    bias3 = bias_full(bias_z2, mask_add)
     d_cols = rows_to_cols(d_pair_blk[0])
     z3 = att_fwd(z2, bias3, w3q, w3o, 4)
     z3, d_cols = tie(z3, d_cols)
     z3 = rows_to_cols(z3)
     bias4 = bias_full(att_bias(z3, w4bt), mask_add)
     z4 = att_fwd(z3, bias4, w4q, w4o, 4).reshape(-1, C)
-    z5 = trans_fwd(z4, wpu, wpd, 1024).reshape(rows, T, C)
-    biass = bias_full(att_bias(z5, wspt), mask_add[:, None])
-
-    s_all, ds_all, dbias_s, g_sb, g_sq, g_so, g_su, g_sd = single_step(both[0], both[1], biass, wsq, wsb[None], wso, wsu, wsd)
+    z5, bias_z5 = trans_fwd(z4, wpu, wpd, wspt)
+    z5 = z5.reshape(rows, T, C)
+    biass = bias_full(bias_z5, mask_add[:, None])
+
+    s_all, ds_all, dbias_s, g_s = single_step(both[0], both[1], biass, wsq, wsb[None], wso, wsu, wsd)
     s_out = lax.dynamic_slice_in_dim(s_all, me * rows, rows)
     ds_in = lax.dynamic_slice_in_dim(ds_all, me * rows, rows)
     dbias_s = jnp.transpose(lax.dynamic_slice_in_dim(dbias_s, me * rows, rows, 1), (1, 0, 2))
-    g_sb = jnp.pad(g_sb.reshape(3, 128), ((0, 5), (0, 0)))
-    half_s = group_half([g_sq, g_so, g_su, g_sd, g_sb], False)
+    half_s = group_half([g_s], False)
     half_s, z5 = tie(half_s, z5)
     part_s = scatter_group(half_s)
 
@@ -851,10 +883,11 @@
     dx1, dgl1, g_1o, dxp = mul_post_bwd(x1, z0, dz1, w1g, w1o, 1)
     half_i, dxp = tie(half_i, dxp)
     part_i = scatter_group(half_i)
-    dxt = flip(lax.all_to_all(dxp, GROUP_AXIS, 1, 0, tiled=True))
-    dab1 = mix_all(functools.partial(mix_bwd_out, idx), dx1, dxt, b1g, a1g)
+    dxt = lax.all_to_all(dxp, GROUP_AXIS, 1, 0, tiled=True)
+    da1 = mix_all(functools.partial(mix_nn, idx), dx1, b1g)
+    db1 = mix_all(functools.partial(mix_nn, idx), flip(dxt), a1g)
     full_i = gather_group(part_i, True)
-    dz0, g_1i, g_1g = mul_pre_bwd(z0, dz1, [d[0] for d in dab1], [d[1] for d in dab1], dgl1, w1i, w1t, w1g)
+    dz0, g_1i, g_1g = mul_pre_bwd(z0, dz1, da1, db1, dgl1, w1i, w1t, w1g)
     half_o = group_half([g_1i, g_1g, g_1o], True)
     full_o = small_group(half_o)
 

time: 1020 us -> 1000 us (0.980)
  waiting for transfers between devices: 321 us -> 307 us
  Pallas kernels: 407 us -> 420 us
    ppermute x21, waiting for transfers between devices: 204 us -> 190 us  [swap_chip(): return lax.ppermute(x_in, GROUP_AXIS, flip_perm(2))]
    unnamed x114 -> x99, local copies, waits for them, and re-layouts: 36.9 us -> 27 us
    pallas_call x16 -> x20, Pallas kernels: 73.1 us -> 82.9 us  [mix_call(): pl.pallas_call(body, grid_spec=gs, out_shape=[jax.ShapeDtypeStruct((w, r,...]
  transfers between devices with their start and end apart: 80 -> 80, of which waited for: 32 -> 31; matrix products, arithmetic and copies ran while one was open for 6% -> 6% of each run, Pallas kernels for 30% -> 31%
where the time goes in v2:
time: 1000 us; the launch traced here: 994 us
  Pallas kernels  420 us (42%)
  waiting for transfers between devices  307 us (31%)
  local copies, waits for them, and re-layouts  107 us (11%)
  starting transfers between devices  83.5 us (8%)
  blocking collectives  46 us (5%)
  other arithmetic  15.2 us (2%)
  between operations  15.1 us (2%)
    ppermute x21, waiting for transfers between devices, swap_chip(): return lax.ppermute(x_in, GROUP_AXIS, flip_perm(2))  190 us
    pallas_call x2, Pallas kernels, att_bwd(): pl.pallas_call(att_bwd_body, grid=(r // b,), in_specs=[spec, spec, full(b...  84.4 us
    pallas_call x20, Pallas kernels, mix_call(): pl.pallas_call(body, grid_spec=gs, out_shape=[jax.ShapeDtypeStruct((w, r,...  82.9 us
    all_to_all x2, waiting for transfers between devices, cols_to_rows(): lax.all_to_all(jnp.transpose(x_in, (1, 0, 2)), GROUP_AXIS, 0, 1, tiled=True)  48.7 us
    pallas_call x2, Pallas kernels, mul_pre_bwd(): pl.pallas_call(mul_pre_bwd_body, grid=(r // RB,), in_specs=cspecs(NCH) *...  37 us
    pallas_call x2, Pallas kernels, mul_post_bwd(): pl.pallas_call(functools.partial(mul_post_bwd_body, pix), grid=(r // RB,)...  36.8 us
    ppermute x41, starting transfers between devices, swap_core(): return lax.ppermute(x_in, GROUP_AXIS, flip_perm(1))  36.7 us
    pallas_call x2, Pallas kernels, att_fwd(): pl.pallas_call(att_fwd_body, grid=(r // b,), in_specs=[spec, full(bias),...  36.6 us
  transfers between devices with their start and end apart: 80, of which 31 were waited for; matrix products, arithmetic and copies ran while one was open for 6% of the time, Pallas kernels for 31%

profile of v2, /device:TPU:5, one launch (start us, length us, event | category | flops | bytes accessed | tf_op | source)
XLA Modules:
  0.0 993.8 jit_solution(15018833481182653371)
XLA Ops:
  22.0 10.0 %collective-permute-done.1.b2 = bf16[64,32,128]{2,1,0:T(8,128)(2,1)S(1)} collective-permute-done((bf16[64,32,128]{2,1,0:T(8,128)(2,1)}, bf16[64,32,128]{2,1,0:T(8,128)(2,1)S(1)}, u32[]{:S(2)}, u32[]{:S(2)}) %collective-permute-start.1) | collective-permute-done | bytes 524320 | tf_op jit(solution)/shard_map/ppermute | solution.py:687
  33.5 9.8 collective-permute-done.4.b2
  44.8 9.7 collective-permute-done.7.b2
  56.0 9.8 collective-permute-done.10.b2
  107.3 19.6 %all-to-all-done = bf16[32,128,256]{2,0,1:T(8,128)(2,1)S(1)} async-done(((bf16[32,128,256]{2,0,1:T(8,128)(2,1)}), bf16[32,128,256]{2,0,1:T(8,128)(2,1)S(1)}, u32[]{:S(2)}, u32[]{:S(2)}) %all-to-all-start) | async-done | bytes 2097184 | tf_op jit(solution)/shard_map/all_to_all | solution.py:707
  149.4 19.4 %collective-permute-done.13.b2 = bf16[64,32,128]{2,1,0:T(8,128)(2,1)S(1)} collective-permute-done((bf16[64,32,128]{2,1,0:T(8,128)(2,1)}, bf16[64,32,128]{2,1,0:T(8,128)(2,1)S(1)}, u32[]{:S(2)}, u32[]{:S(2)}) %collective-permute-start.13) | collective-permute-done | bytes 524320 | tf_op jit(solution)/shard_map/ppermute | solution.py:687
  170.4 9.8 collective-permute-done.16.b2
  192.9 9.7 collective-permute-done.22.b2
  223.0 17.7 %mul_post.3 = (bf16[32,128,256]{2,1,0:T(8,128)(2,1)}, bf16[32,8,128]{2,1,0:T(8,128)(2,1)}) custom-call(f32[64,32,128]{2,1,0:T(8,128)} %shard_map.276.refs_0_, f32[64,32,128]{2,1,0:T(8,128)} %shard_map.277.refs_1_, f32[64,32,128]{2,1,0:T(8,128)} %shard_map.278.refs_2_, f32[64,32,128]{2,1,0:T(8,128)} %shard_map.279.refs_3_, ...), custom_call_target="tpu_custom_call" | custom-call | flops 4294967296 | bytes 8388608 | tf_op jit(solution)/shard_map/mul_post/pallas_call | solution.py:489
  248.4 18.3 %att_fwd.2 = bf16[32,128,256]{2,1,0:T(8,128)(2,1)} custom-call(bf16[32,128,256]{2,1,0:T(8,128)(2,1)} %get-tuple-element.234.z_ref, f32[8,128,128]{2,1,0:T(8,128)} %add_bitcast_fusion.2.bias_ref, bf16[256,1024]{1,0:T(8,128)(2,1)} %wq_ref.9, bf16[256,256]{1,0:T(8,128)(2,1)} %wo_ref.9), custom_call_target="tpu_custom_call" | custom-call | flops 4294967296 | bytes 8388608 | tf_op jit(solution)/shard_map/att_fwd/pallas_call | solution.py:240
  275.7 26.8 %all_gather.27 = bf16[2,128,384]{2,1,0:T(8,128)(2,1)S(1)} all-gather(bf16[2,32,384]{2,1,0:T(8,128)(2,1)S(1)} %pad_maximum_fusion.2), channel_id=1, replica_groups=mesh['dp'=8,'dap'=4] {'dap'}, dimensions={1}, use_global_device_ids=true | all-gather | bytes 245760 | tf_op jit(solution)/shard_map/all_gather | solution.py:828
  316.8 18.3 %att_fwd.3 = bf16[32,128,256]{2,1,0:T(8,128)(2,1)} custom-call(bf16[32,128,256]{2,1,0:T(8,128)(2,1)} %bitcast.204, f32[8,128,128]{2,1,0:T(8,128)} %add_bitcast_fusion.1.bias_ref, bf16[256,1024]{1,0:T(8,128)(2,1)} %wq_ref.8, bf16[256,256]{1,0:T(8,128)(2,1)} %wo_ref.8), custom_call_target="tpu_custom_call" | custom-call | flops 4294967296 | bytes 8388608 | tf_op jit(solution)/shard_map/att_fwd/pallas_call | solution.py:240
  335.1 14.1 %trans_fwd.1 = (bf16[4096,256]{1,0:T(8,128)(2,1)}, bf16[32,16,128]{2,1,0:T(8,128)(2,1)}) custom-call(bf16[4096,256]{1,0:T(8,128)(2,1)} %bitcast.238, bf16[256,2048]{1,0:T(8,128)(2,1)} %wu_ref.5, bf16[1024,256]{1,0:T(8,128)(2,1)} %wd_ref.5, bf16[16,256]{1,0:T(8,128)(2,1)} %bitcast.231), custom_call_target="tpu_custom_call" | custom-call | flops 4294967296 | bytes 8388608 | tf_op jit(solution)/shard_map/trans_fwd/pallas_call | solution.py:144
  358.7 14.3 %single_step.1 = (bf16[128,384]{1,0:T(8,128)(2,1)}, bf16[128,384]{1,0:T(8,128)(2,1)}, f32[16,128,128]{2,1,0:T(8,128)}, f32[19712,128]{1,0:T(8,128)}) custom-call(bf16[128,384]{1,0:T(8,128)(2,1)} %get-tuple-element.321.s_ref, bf16[128,384]{1,0:T(8,128)(2,1)} %get-tuple-element.320.d_ref, f32[16,128,128]{2,1,0:T(8,128)} %add_bitcast_fusion.bias_ref, ...), custom_call_target="tpu_custom_call" | custom-call | flops 8589934592 | bytes 16777216 | tf_op jit(solution)/shard_map/single_step/pallas_call | solution.py:673
  386.4 30.1 %trans_bwd.1 = (bf16[4096,256]{1,0:T(8,128)(2,1)}, f32[4096,128]{1,0:T(8,128)}, f32[2048,128]{1,0:T(8,128)}) custom-call(bf16[4096,256]{1,0:T(8,128)(2,1)} %bitcast.239, bf16[4096,256]{1,0:T(8,128)(2,1)} %bitcast.242, bf16[256,2048]{1,0:T(8,128)(2,1)} %wu_ref.5, bf16[1024,256]{1,0:T(8,128)(2,1)} %wd_ref.5), custom_call_target="tpu_custom_call" | custom-call | flops 4294967296 | bytes 8388608 | tf_op jit(solution)/shard_map/trans_bwd/pallas_call | solution.py:151
  416.6 42.2 %att_bwd.2 = (f32[4096,256]{1,0:T(8,128)}, f32[8,128,128]{2,1,0:T(8,128)}, f32[2048,128]{1,0:T(8,128)}, f32[512,128]{1,0:T(8,128)}) custom-call(bf16[32,128,256]{2,1,0:T(8,128)(2,1)} %bitcast.205, bf16[32,128,256]{2,1,0:T(8,128)(2,1)} %bitcast.240, f32[8,128,128]{2,1,0:T(8,128)} %add_bitcast_fusion.1.bias_ref, bf16[256,1024]{1,0:T(8,128)(2,1)} %wq_ref.8, ...), custom_call_target="tpu_custom_call" | custom-call | flops 4294967296 | bytes 8388608 | tf_op jit(solution)/shard_map/att_bwd/pallas_call | solution.py:311
  491.7 24.7 %all-to-all-done.3 = bf16[128,32,256]{2,1,0:T(8,128)(2,1)S(1)} async-done(((bf16[128,32,256]{2,1,0:T(8,128)(2,1)}), bf16[128,32,256]{2,1,0:T(8,128)(2,1)S(1)}, u32[]{:S(2)}, u32[]{:S(2)}) %all-to-all-start.3) | async-done | bytes 2097184 | tf_op jit(solution)/shard_map/all_to_all | solution.py:711
  531.3 24.0 %all-to-all-done.4 = bf16[128,32,256]{2,1,0:T(8,128)(2,1)S(1)} async-done(((bf16[128,32,256]{2,1,0:T(8,128)(2,1)}), bf16[128,32,256]{2,1,0:T(8,128)(2,1)S(1)}, u32[]{:S(2)}, u32[]{:S(2)}) %all-to-all-start.4) | async-done | bytes 2097184 | tf_op jit(solution)/shard_map/all_to_all | solution.py:711
  556.9 42.1 %att_bwd.3 = (f32[4096,256]{1,0:T(8,128)}, f32[8,128,128]{2,1,0:T(8,128)}, f32[2048,128]{1,0:T(8,128)}, f32[512,128]{1,0:T(8,128)}) custom-call(bf16[32,128,256]{2,1,0:T(8,128)(2,1)} %get-tuple-element.234.z_ref, bf16[32,128,256]{2,1,0:T(8,128)(2,1)} %bitcast.207, f32[8,128,128]{2,1,0:T(8,128)} %add_bitcast_fusion.2.bias_ref, bf16[256,1024]{1,0:T(8,128)(2,1)} %wq_ref.9, ...), custom_call_target="tpu_custom_call" | custom-call | flops 4294967296 | bytes 8388608 | tf_op jit(solution)/shard_map/att_bwd/pallas_call | solution.py:311
  618.4 18.0 %mul_post_bwd.2 = (bf16[64,32,128]{2,1,0:T(8,128)(2,1)}, bf16[64,32,128]{2,1,0:T(8,128)(2,1)}, bf16[64,32,128]{2,1,0:T(8,128)(2,1)}, bf16[64,32,128]{2,1,0:T(8,1...) custom-call(f32[64,32,128]{2,1,0:T(8,128)} %shard_map.276.refs_0_, f32[64,32,128]{2,1,0:T(8,128)} %shard_map.277.refs_1_, ...), custom_call_target="tpu_custom_call" | custom-call | flops 4294967296 | bytes 8388608 | tf_op jit(solution)/shard_map/mul_post_bwd/pallas_call | solution.py:527
  640.3 10.2 %collective-permute-done.30.d2 = bf16[64,32,128]{2,1,0:T(8,128)(2,1)} collective-permute-done((bf16[64,32,128]{2,1,0:T(8,128)(2,1)}, bf16[64,32,128]{2,1,0:T(8,128)(2,1)}, u32[]{:S(2)}, u32[]{:S(2)}) %collective-permute-start.30) | collective-permute-done | bytes 524320 | tf_op jit(solution)/shard_map/ppermute | solution.py:687
  663.4 9.6 collective-permute-done.36.d2
  705.4 18.4 %mul_pre_bwd.2 = (bf16[32,128,256]{2,1,0:T(8,128)(2,1)}, f32[2048,128]{1,0:T(8,128)}, f32[512,128]{1,0:T(8,128)}) custom-call(bf16[64,32,128]{2,1,0:T(8,128)(2,1)} %get-tuple-element.265.refs_0_, bf16[64,32,128]{2,1,0:T(8,128)(2,1)} %get-tuple-element.269.refs_1_, bf16[64,32,128]{2,1,0:T(8,128)(2,1)} %get-tuple-element.273.refs_2_, ...), custom_call_target="tpu_custom_call" | custom-call | flops 4294967296 | bytes 8388608 | tf_op jit(solution)/shard_map/mul_pre_bwd/pallas_call | solution.py:596
  727.9 18.8 %mul_post_bwd.3 = (bf16[64,32,128]{2,1,0:T(8,128)(2,1)}, bf16[64,32,128]{2,1,0:T(8,128)(2,1)}, bf16[64,32,128]{2,1,0:T(8,128)(2,1)}, bf16[64,32,128]{2,1,0:T(8,1...) custom-call(f32[64,32,128]{2,1,0:T(8,128)} %shard_map.272.refs_0_, ...), custom_call_target="tpu_custom_call" | custom-call | flops 4294967296 | bytes 8388608 | tf_op jit(solution)/shard_map/mul_post_bwd/pallas_call | solution.py:527
  758.6 29.4 %collective-permute-done.65 = f32[552,128]{1,0:T(8,128)S(1)} collective-permute-done((f32[552,128]{1,0:T(8,128)}, f32[552,128]{1,0:T(8,128)S(1)}, u32[]{:S(2)}, u32[]{:S(2)}) %collective-permute-start.65) | collective-permute-done | bytes 282656 | tf_op jit(solution)/shard_map/ppermute | solution.py:687
  794.4 10.1 %collective-permute-done.43.b2 = bf16[64,32,128]{2,1,0:T(8,128)(2,1)} collective-permute-done((bf16[64,32,128]{2,1,0:T(8,128)(2,1)}, bf16[64,32,128]{2,1,0:T(8,128)(2,1)}, u32[]{:S(2)}, u32[]{:S(2)}) %collective-permute-start.43) | collective-permute-done | bytes 524320 | tf_op jit(solution)/shard_map/ppermute | solution.py:687
  828.5 9.8 collective-permute-done.52.b2
  860.7 18.5 %mul_pre_bwd.3 = (bf16[32,128,256]{2,1,0:T(8,128)(2,1)}, f32[2048,128]{1,0:T(8,128)}, f32[512,128]{1,0:T(8,128)}) custom-call(bf16[64,32,128]{2,1,0:T(8,128)(2,1)} %shard_map.284.refs_0_, bf16[64,32,128]{2,1,0:T(8,128)(2,1)} %shard_map.285.refs_1_, bf16[64,32,128]{2,1,0:T(8,128)(2,1)} %shard_map.286.refs_2_, bf16[64,32,128]{2,1,0:T(8,128)(2,1)} %shard_map.287.refs_3_, ...), custom_call_target="tpu_custom_call" | custom-call | flops 4294967296 | bytes 8388608 | tf_op jit(solution)/shard_map/mul_pre_bwd/pallas_call | solution.py:596
  920.3 11.6 %collective-permute-done.59 = f32[192,128]{1,0:T(8,128)S(1)} collective-permute-done((f32[192,128]{1,0:T(8,128)S(1)}, f32[192,128]{1,0:T(8,128)S(1)}, u32[]{:S(2)}, u32[]{:S(2)}) %collective-permute-start.59) | collective-permute-done | bytes 98336 | tf_op jit(solution)/shard_map/ppermute | solution.py:768
  942.1 9.6 collective-permute-done.61
  955.5 31.2 %conditional.1 = (f32[592944]{0:T(1024)}) conditional(s32[]{:T(128)} %clamp.3, (f32[1536,128]{1,0:T(8,128)S(1)}, f32[1536,128]{1,0:T(8,128)}, f32[2880,128]{1,0:T(8,128)}, f32[2880,128]{1,0:T(8,128)}) %tuple.66, (f32[1536,128]{1,0:T(8,128)}, f32[1536,128]{1,0:T(8,128)S(1)}, f32[2880,128]{1,0:T(8,128)}, ...), branch_computations={%region_3.4_spmd, %region_4.5_spmd, %region_5.6_spmd, %region_6.7_... | conditional | flops 592944 | bytes 15434532 | solution.py:810
  962.4 24.2 %concatenate.37 = f32[592944]{0:T(1024)} concatenate(f32[62416]{0:T(1024)} %slice.282, f32[65536]{0:T(1024)} %get-tuple-element.314, f32[65536]{0:T(1024)} %get-tuple-element.313, f32[262144]{0:T(1024)S(1)} %slice_bitcast_fusion.4, f32[2048]{0:T(1024)S(1)} %reshape.209, f32[65536]{0:T(1024)} %get-tuple-element.315, f32[69728]{0:T(1024)} %slice.283), dimensions={0} | concatenate | bytes 4743552 | tf_op jit(solution)/shard_map/cond/branch_3_fun/concatenate | solution.py:804
  (353 shorter events, 419.6 us)
Async XLA Ops:
  20.5 34.0 %collective-permute-start.7 = (bf16[64,32,128]{2,1,0:T(8,128)(2,1)}, bf16[64,32,128]{2,1,0:T(8,128)(2,1)S(1)}, u32[]{:S(2)}, u32[]{:S(2)}) collective-permute-start(bf16[64,32,128]{2,1,0:T(8,128)(2,1)} %get-tuple-element.223.b0), channel_id=1, source_target_pairs={{0,2},{1,3},{2,0},{3,1},{4,6},{5,7},{6,4},{7,5},{8,10},{9,11},{10,... | collective-permute-start | bytes 1572872 | tf_op jit(solution)/shard_map/ppermute | solution.py:687
  21.7 44.0 %collective-permute-start.10 = (bf16[64,32,128]{2,1,0:T(8,128)(2,1)}, bf16[64,32,128]{2,1,0:T(8,128)(2,1)S(1)}, u32[]{:S(2)}, u32[]{:S(2)}) collective-permute-start(bf16[64,32,128]{2,1,0:T(8,128)(2,1)} %get-tuple-element.225.b0), channel_id=1, source_target_pairs={{0,2},{1,3},{2,0},{3,1},{4,6},{5,7},{6,4},{7,5},{8,10},{9,11},{10,... | collective-permute-start | bytes 1572872 | tf_op jit(solution)/shard_map/ppermute | solution.py:687
  32.0 34.6 %collective-permute-start.2 = (bf16[64,32,128]{2,1,0:T(8,128)(2,1)S(1)}, bf16[64,32,128]{2,1,0:T(8,128)(2,1)S(1)}, u32[]{:S(2)}, u32[]{:S(2)}) collective-permute-start(bf16[64,32,128]{2,1,0:T(8,128)(2,1)S(1)} %collective-permute-done.1.b2), channel_id=1, source_target_pairs={{0,1},{1,0},{2,3},{3,2},{4,5},{5,4},{6,7},{7,6},{8,9},{9,8},{10,11... | collective-permute-start | bytes 1572872 | tf_op jit(solution)/shard_map/ppermute | solution.py:683
  44.7 31.7 %collective-permute-start.6 = (bf16[64,32,128]{2,1,0:T(8,128)(2,1)}, bf16[64,32,128]{2,1,0:T(8,128)(2,1)}, u32[]{:S(2)}, u32[]{:S(2)}) collective-permute-start(bf16[64,32,128]{2,1,0:T(8,128)(2,1)} %get-tuple-element.223.b0), channel_id=1, source_target_pairs={{0,1},{1,0},{2,3},{3,2},{4,5},{5,4},{6,7},{7,6},{8,9},{9,8},{10,11... | collective-permute-start | bytes 1572872 | tf_op jit(solution)/shard_map/ppermute | solution.py:683
  128.2 76.2 %all-to-all-start.1 = ((bf16[32,128,256]{2,0,1:T(8,128)(2,1)}), bf16[32,128,256]{2,0,1:T(8,128)(2,1)S(1)}, u32[]{:S(2)}, u32[]{:S(2)}) async-start(bf16[32,128,256]{2,0,1:T(8,128)(2,1)} %bitcast.177), calls=%async_computation.1 | async-start | bytes 4194304 | tf_op jit(solution)/shard_map/all_to_all | solution.py:707
  146.4 33.8 %collective-permute-start.16 = (bf16[64,32,128]{2,1,0:T(8,128)(2,1)}, bf16[64,32,128]{2,1,0:T(8,128)(2,1)}, u32[]{:S(2)}, u32[]{:S(2)}) collective-permute-start(bf16[64,32,128]{2,1,0:T(8,128)(2,1)} %get-tuple-element.229.b0), channel_id=1, source_target_pairs={{0,2},{1,3},{2,0},{3,1},{4,6},{5,7},{6,4},{7,5},{8,10},{9,11},{10,... | collective-permute-start | bytes 1572872 | tf_op jit(solution)/shard_map/ppermute | solution.py:687
  146.4 35.4 %collective-permute-start.15 = (bf16[64,32,128]{2,1,0:T(8,128)(2,1)}, bf16[64,32,128]{2,1,0:T(8,128)(2,1)S(1)}, u32[]{:S(2)}, u32[]{:S(2)}) collective-permute-start(bf16[64,32,128]{2,1,0:T(8,128)(2,1)} %get-tuple-element.229.b0), channel_id=1, source_target_pairs={{0,1},{1,0},{2,3},{3,2},{4,5},{5,4},{6,7},{7,6},{8,9},{9,8},{10,11... | collective-permute-start | bytes 1572872 | tf_op jit(solution)/shard_map/ppermute | solution.py:683
  147.2 44.2 %collective-permute-start.19 = (bf16[64,32,128]{2,1,0:T(8,128)(2,1)}, bf16[64,32,128]{2,1,0:T(8,128)(2,1)S(1)}, u32[]{:S(2)}, u32[]{:S(2)}) collective-permute-start(bf16[64,32,128]{2,1,0:T(8,128)(2,1)} %get-tuple-element.231.b0), channel_id=1, source_target_pairs={{0,2},{1,3},{2,0},{3,1},{4,6},{5,7},{6,4},{7,5},{8,10},{9,11},{10,... | collective-permute-start | bytes 1572872 | tf_op jit(solution)/shard_map/ppermute | solution.py:687
  149.3 53.3 %collective-permute-start.22 = (bf16[64,32,128]{2,1,0:T(8,128)(2,1)}, bf16[64,32,128]{2,1,0:T(8,128)(2,1)S(1)}, u32[]{:S(2)}, u32[]{:S(2)}) collective-permute-start(bf16[64,32,128]{2,1,0:T(8,128)(2,1)} %get-tuple-element.233.b0), channel_id=1, source_target_pairs={{0,2},{1,3},{2,0},{3,1},{4,6},{5,7},{6,4},{7,5},{8,10},{9,11},{10,... | collective-permute-start | bytes 1572872 | tf_op jit(solution)/shard_map/ppermute | solution.py:687
  168.9 34.7 %collective-permute-start.14 = (bf16[64,32,128]{2,1,0:T(8,128)(2,1)S(1)}, bf16[64,32,128]{2,1,0:T(8,128)(2,1)S(1)}, u32[]{:S(2)}, u32[]{:S(2)}) collective-permute-start(bf16[64,32,128]{2,1,0:T(8,128)(2,1)S(1)} %collective-permute-done.13.b2), channel_id=1, source_target_pairs={{0,1},{1,0},{2,3},{3,2},{4,5},{5,4},{6,7},{7,6},{8,9},{9,8},{10,11... | collective-permute-start | bytes 1572872 | tf_op jit(solution)/shard_map/ppermute | solution.py:683
  181.8 32.7 %collective-permute-start.18 = (bf16[64,32,128]{2,1,0:T(8,128)(2,1)}, bf16[64,32,128]{2,1,0:T(8,128)(2,1)}, u32[]{:S(2)}, u32[]{:S(2)}) collective-permute-start(bf16[64,32,128]{2,1,0:T(8,128)(2,1)} %get-tuple-element.231.b0), channel_id=1, source_target_pairs={{0,1},{1,0},{2,3},{3,2},{4,5},{5,4},{6,7},{7,6},{8,9},{9,8},{10,11... | collective-permute-start | bytes 1572872 | tf_op jit(solution)/shard_map/ppermute | solution.py:683
  270.8 32.4 %all-to-all-start.2 = ((bf16[32,128,256]{2,0,1:T(8,128)(2,1)}), bf16[32,128,256]{2,0,1:T(8,128)(2,1)S(1)}, u32[]{:S(2)}, u32[]{:S(2)}) async-start(bf16[32,128,256]{2,0,1:T(8,128)(2,1)} %copy.81), calls=%async_computation.2 | async-start | bytes 4194304 | tf_op jit(solution)/shard_map/all_to_all | solution.py:707
  275.1 255.4 %reduce-scatter.8.cloned.1.call-start = ((), (), s32[]{:S(2)}) async-start(), calls=%async_computation.11 | async-start | bytes 5677056 | tf_op jit(solution)/shard_map/reduce_scatter | solution.py:741
  485.1 32.9 %collective-permute-start.26 = (f32[4416,128]{1,0:T(8,128)}, f32[4416,128]{1,0:T(8,128)}, u32[]{:S(2)}, u32[]{:S(2)}) collective-permute-start(f32[4416,128]{1,0:T(8,128)} %constant_dynamic-slice_fusion.7), channel_id=1, source_target_pairs={{0,1},{1,0},{2,3},{3,2},{4,5},{5,4},{6,7},{7,6},{8,9},{9,8},{10,11... | collective-permute-start | bytes 6782984 | tf_op jit(solution)/shard_map/ppermute | solution.py:683
  491.7 265.6 %reduce-scatter.12.cloned.1.call-start = ((), (), s32[]{:S(2)}) async-start(), calls=%async_computation.14 | async-start | bytes 2543616
  530.6 351.7 %all-gather.8.cloned.1.call-start = ((), (), s32[]{:S(2)}) async-start(), calls=%async_computation.12 | async-start | bytes 5677056 | tf_op jit(solution)/shard_map/all_gather | solution.py:747
  531.3 351.1 %reduce-scatter.10.cloned.1.call-start = ((), (), s32[]{:S(2)}) async-start(), calls=%async_computation.13 | async-start | bytes 1658880
  638.8 34.2 %collective-permute-start.36 = (bf16[64,32,128]{2,1,0:T(8,128)(2,1)}, bf16[64,32,128]{2,1,0:T(8,128)(2,1)}, u32[]{:S(2)}, u32[]{:S(2)}) collective-permute-start(bf16[64,32,128]{2,1,0:T(8,128)(2,1)} %get-tuple-element.272.d0), channel_id=1, source_target_pairs={{0,2},{1,3},{2,0},{3,1},{4,6},{5,7},{6,4},{7,5},{8,10},{9,11},{10,... | collective-permute-start | bytes 1572872 | tf_op jit(solution)/shard_map/ppermute | solution.py:687
  639.1 45.1 %collective-permute-start.39 = (bf16[64,32,128]{2,1,0:T(8,128)(2,1)}, bf16[64,32,128]{2,1,0:T(8,128)(2,1)}, u32[]{:S(2)}, u32[]{:S(2)}) collective-permute-start(bf16[64,32,128]{2,1,0:T(8,128)(2,1)} %get-tuple-element.276.d0), channel_id=1, source_target_pairs={{0,2},{1,3},{2,0},{3,1},{4,6},{5,7},{6,4},{7,5},{8,10},{9,11},{10,... | collective-permute-start | bytes 1572872 | tf_op jit(solution)/shard_map/ppermute | solution.py:687
  650.5 34.7 %collective-permute-start.31 = (bf16[64,32,128]{2,1,0:T(8,128)(2,1)}, bf16[64,32,128]{2,1,0:T(8,128)(2,1)}, u32[]{:S(2)}, u32[]{:S(2)}) collective-permute-start(bf16[64,32,128]{2,1,0:T(8,128)(2,1)} %collective-permute-done.30.d2), channel_id=1, source_target_pairs={{0,1},{1,0},{2,3},{3,2},{4,5},{5,4},{6,7},{7,6},{8,9},{9,8},{10,11... | collective-permute-start | bytes 1572872 | tf_op jit(solution)/shard_map/ppermute | solution.py:683
  660.7 34.6 %collective-permute-start.35 = (bf16[64,32,128]{2,1,0:T(8,128)(2,1)}, bf16[64,32,128]{2,1,0:T(8,128)(2,1)}, u32[]{:S(2)}, u32[]{:S(2)}) collective-permute-start(bf16[64,32,128]{2,1,0:T(8,128)(2,1)} %get-tuple-element.272.d0), channel_id=1, source_target_pairs={{0,1},{1,0},{2,3},{3,2},{4,5},{5,4},{6,7},{7,6},{8,9},{9,8},{10,11... | collective-permute-start | bytes 1572872 | tf_op jit(solution)/shard_map/ppermute | solution.py:683
  753.5 67.3 %all-to-all-start.5 = ((bf16[32,128,256]{2,0,1:T(8,128)(2,1)}), bf16[32,128,256]{2,0,1:T(8,128)(2,1)S(1)}, u32[]{:S(2)}, u32[]{:S(2)}) async-start(bf16[32,128,256]{2,0,1:T(8,128)(2,1)} %copy.94), calls=%async_computation.5 | async-start | bytes 4194304 | tf_op jit(solution)/shard_map/all_to_all | solution.py:886
  757.3 154.7 %all-gather.6.cloned.1.call-start = ((), (), s32[]{:S(2)}) async-start(), calls=%async_computation.10 | async-start | bytes 2543616 | tf_op jit(solution)/shard_map/all_gather | solution.py:747
  757.3 30.7 %collective-permute-start.65 = (f32[552,128]{1,0:T(8,128)}, f32[552,128]{1,0:T(8,128)S(1)}, u32[]{:S(2)}, u32[]{:S(2)}) collective-permute-start(f32[552,128]{1,0:T(8,128)} %reduce-scatter.12.cloned.1.call-done), channel_id=1, source_target_pairs={{0,2},{1,3},{2,0},{3,1},{4,6},{5,7},{6,4},{7,5},{8,10},{9,11},{10,... | collective-permute-start | bytes 847880 | tf_op jit(solution)/shard_map/ppermute | solution.py:687
  789.8 149.9 %all-gather.4.cloned.1.call-start = ((), (), s32[]{:S(2)}) async-start(), calls=%async_computation.9 | async-start | bytes 1658880 | tf_op jit(solution)/shard_map/all_gather | solution.py:747
  792.3 31.0 %collective-permute-start.45 = (bf16[64,32,128]{2,1,0:T(8,128)(2,1)}, bf16[64,32,128]{2,1,0:T(8,128)(2,1)}, u32[]{:S(2)}, u32[]{:S(2)}) collective-permute-start(bf16[64,32,128]{2,1,0:T(8,128)(2,1)} %get-tuple-element.220.a_ref.b0), channel_id=1, source_target_pairs={{0,1},{1,0},{2,3},{3,2},{4,5},{5,4},{6,7},{7,6},{8,9},{9,8},{10,11... | collective-permute-start | bytes 1572872 | tf_op jit(solution)/shard_map/ppermute | solution.py:683
  793.0 34.1 %collective-permute-start.49 = (bf16[64,32,128]{2,1,0:T(8,128)(2,1)S(1)}, bf16[64,32,128]{2,1,0:T(8,128)(2,1)}, u32[]{:S(2)}, u32[]{:S(2)}) collective-permute-start(bf16[64,32,128]{2,1,0:T(8,128)(2,1)S(1)} %copy-done.20), channel_id=1, source_target_pairs={{0,2},{1,3},{2,0},{3,1},{4,6},{5,7},{6,4},{7,5},{8,10},{9,11},{10,... | collective-permute-start | bytes 1572872 | tf_op jit(solution)/shard_map/ppermute | solution.py:687
  793.1 45.2 %collective-permute-start.52 = (bf16[64,32,128]{2,1,0:T(8,128)(2,1)S(1)}, bf16[64,32,128]{2,1,0:T(8,128)(2,1)}, u32[]{:S(2)}, u32[]{:S(2)}) collective-permute-start(bf16[64,32,128]{2,1,0:T(8,128)(2,1)S(1)} %copy-done.19), channel_id=1, source_target_pairs={{0,2},{1,3},{2,0},{3,1},{4,6},{5,7},{6,4},{7,5},{8,10},{9,11},{10,... | collective-permute-start | bytes 1572872 | tf_op jit(solution)/shard_map/ppermute | solution.py:687
  804.6 34.6 %collective-permute-start.44 = (bf16[64,32,128]{2,1,0:T(8,128)(2,1)}, bf16[64,32,128]{2,1,0:T(8,128)(2,1)}, u32[]{:S(2)}, u32[]{:S(2)}) collective-permute-start(bf16[64,32,128]{2,1,0:T(8,128)(2,1)} %collective-permute-done.43.b2), channel_id=1, source_target_pairs={{0,1},{1,0},{2,3},{3,2},{4,5},{5,4},{6,7},{7,6},{8,9},{9,8},{10,11... | collective-permute-start | bytes 1572872 | tf_op jit(solution)/shard_map/ppermute | solution.py:683
  817.2 30.8 %collective-permute-start.47 = (bf16[64,32,128]{2,1,0:T(8,128)(2,1)}, bf16[64,32,128]{2,1,0:T(8,128)(2,1)}, u32[]{:S(2)}, u32[]{:S(2)}) collective-permute-start(bf16[64,32,128]{2,1,0:T(8,128)(2,1)} %collective-permute-done.46.b2), channel_id=1, source_target_pairs={{0,1},{1,0},{2,3},{3,2},{4,5},{5,4},{6,7},{7,6},{8,9},{9,8},{10,11... | collective-permute-start | bytes 1572872 | tf_op jit(solution)/shard_map/ppermute | solution.py:683
  882.2 73.2 %collective-permute-start.67 = (f32[9856,128]{1,0:T(8,128)}, f32[9856,128]{1,0:T(8,128)}, u32[]{:S(2)}, u32[]{:S(2)}) collective-permute-start(f32[9856,128]{1,0:T(8,128)} %all-gather.8.cloned.1.call-done), channel_id=1, source_target_pairs={{0,1},{1,0},{2,3},{3,2},{4,5},{5,4},{6,7},{7,6},{8,9},{9,8},{10,11... | collective-permute-start | bytes 15138824 | tf_op jit(solution)/shard_map/ppermute | solution.py:683
  911.9 43.5 %collective-permute-start.66 = (f32[4416,128]{1,0:T(8,128)}, f32[4416,128]{1,0:T(8,128)}, u32[]{:S(2)}, u32[]{:S(2)}) collective-permute-start(f32[4416,128]{1,0:T(8,128)} %all-gather.6.cloned.1.call-done), channel_id=1, source_target_pairs={{0,1},{1,0},{2,3},{3,2},{4,5},{5,4},{6,7},{7,6},{8,9},{9,8},{10,11... | collective-permute-start | bytes 6782984 | tf_op jit(solution)/shard_map/ppermute | solution.py:683
  (89 other events, 1461.0 us)
Sparse Core Ops, SparseCore 0:
  377.4 100.2 reduce-scatter.7
  522.1 67.2 reduce-scatter.11
  591.6 82.2 all-gather.7
  749.5 61.6 reduce-scatter.9
  813.2 49.2 all-gather.5
  890.1 49.5 all-gather.3
